TPU v7x, 32 devices: a whole 2x2x4 slice. The times are simulated.
32 devices in a mesh: section: 8 (over z, x), tensor: 4 (over y, core).
Axes of the slice: x: 2, y: 2, z: 4, core: 2. Of those that a mesh axis runs over, the one named last changes fastest.
Arguments:
- hidden: bfloat16 [32, 8192], P(('section', 'tensor')), may hold values from -12 to 12
- weight: bfloat16 [16384, 8192], P(('section', 'tensor')), may hold values from -1 to 1
- targets: int32 [32], replicated, may hold values from 0 to 16383
- loss_grad: float32 [32], P(('section', 'tensor')), may hold values from 8 to 64
Outputs:
- token_loss: float32 [32], P(('section', 'tensor'))
- hidden_grad: bfloat16 [32, 8192], P(('section', 'tensor'))
All inputs are finite; a program needn't handle non-finite values.
Results may differ from a plain program's by a relative error of at most 0.0039.
Values may be sent and summed in bfloat16 or wider, within the bound.
No kernel may reach another device: no remote copies, remote signals or barrier semaphores. Data moves between devices by JAX's collectives and lax.ppermute only.
A program may use at most 64 MiB of HBM per device.

v0:
```python
import jax
import jax.numpy as jnp
from jax import lax
from jax.sharding import PartitionSpec as P


def joined(array, axis, combine):
    everything = jax.tree.map(lambda part: lax.all_gather(part, axis), array)
    initial = jax.tree.map(lambda part: part[0], everything)

    def lap(k, so_far):
        return combine(so_far, jax.tree.map(lambda part: part[k], everything))

    return lax.fori_loop(1, lax.axis_size(axis), lap, initial)


def combine_parts(left_part, right_part):
    largest = jnp.maximum(left_part[0], right_part[0])
    summed = left_part[1] * jnp.exp(left_part[0] - largest) + right_part[1] * jnp.exp(
        right_part[0] - largest
    )
    return (largest, summed, left_part[2] + right_part[2])


def shards(hidden, weight, targets, loss_grad):
    tok_dev = hidden.shape[0]
    vocab_dev = weight.shape[0]
    logits = lax.dot_general(
        lax.all_gather(hidden, ("section", "tensor"), axis=0, tiled=True),
        weight,
        (((1,), (1,)), ((), ())),
        preferred_element_type=jnp.float32,
    )
    my_index = lax.axis_index(("section", "tensor"))
    offset = my_index * vocab_dev
    columns = offset + lax.broadcasted_iota(jnp.int32, (1, vocab_dev), 1)
    target_mask = columns == targets[:, None]
    local_target = jnp.sum(jnp.where(target_mask, logits, 0.0), axis=1)
    local_max = jnp.max(logits, axis=1)
    local_shift = jnp.exp(logits - local_max[:, None])
    local_total = jnp.sum(local_shift, axis=1)
    row_max, exp_total, target_logit = joined(
        (local_max, local_total, local_target), ("section", "tensor"), combine_parts
    )
    shifted = local_shift * jnp.exp(local_max - row_max)[:, None]
    probs_grad = (shifted / exp_total[:, None] - target_mask.astype(jnp.float32)).astype(
        jnp.bfloat16
    )
    all_loss = row_max + jnp.log(exp_total) - target_logit
    token_loss = lax.dynamic_slice_in_dim(all_loss, my_index * tok_dev, tok_dev)
    grad_sum = lax.psum_scatter(
        jnp.dot(probs_grad, weight, preferred_element_type=jnp.float32),
        ("section", "tensor"),
        scatter_dimension=0,
        tiled=True,
    )
    hidden_grad = (loss_grad[:, None] * grad_sum).astype(jnp.bfloat16)
    return (token_loss, hidden_grad)


def solution(mesh):
    return jax.shard_map(
        shards,
        mesh=mesh,
        in_specs=(
            P(("section", "tensor"), None),
            P(("section", "tensor"), None),
            P(),
            P(("section", "tensor")),
        ),
        out_specs=(P(("section", "tensor")), P(("section", "tensor"), None)),
        check_vma=False,
    )
```

profile of v0, /device:TPU:0, one launch (start us, length us, event | category | flops | bytes accessed | tf_op | source)
XLA Modules:
  0.0 245.1 jit_solution(3485604667387452103)
XLA Ops:
  7.2 0.0 copy-start
  7.2 0.0 all-reduce.7.cloned.1.call-start
  7.2 46.4 %all-gather.3 = bf16[32,1,8192]{2,1,0:T(2,128)(2,1)S(1)} all-gather(bf16[1,1,8192]{2,1,0:T(2,128)(2,1)} %bitcast.29), channel_id=1, replica_groups=mesh['section'=8,'tensor'=4] {'section','tensor'}, dimensions={0}, use_global_device_ids=true | all-gather | bytes 540672 | tf_op jit(solution)/shard_map/all_gather | solution.py:29
  53.6 6.1 %fusion.23 = (f32[32]{0:T(128)S(1)}, f32[32,512]{1,0:T(8,128)S(1)}) fusion(bf16[512,8192]{1,0:T(8,128)(2,1)} %param.7, bf16[32,1,8192]{2,1,0:T(2,128)(2,1)S(1)} %all-gather.3), kind=kOutput, calls=%fused_computation.31 | convolution fusion | flops 268451808 | bytes 8978560 | tf_op jit(solution)/shard_map/dot_general | solution.py:28
  59.7 0.2 dynamic-update-slice
  60.0 0.0 copy-done
  60.0 0.2 fusion.10
  60.2 0.2 dynamic-update-slice.1
  60.4 0.2 dynamic-update-slice.2
  60.6 37.0 %all-reduce.4 = (f32[1024]{0:T(1024)S(1)}, f32[1024]{0:T(1024)S(1)}, f32[1024]{0:T(1024)S(1)}) all-reduce(f32[1024]{0:T(1024)S(1)} %dynamic-update-slice, f32[1024]{0:T(1024)S(1)} %dynamic-update-slice.1, f32[1024]{0:T(1024)S(1)} %dynamic-update-slice.2), channel_id=2, replica_groups=mesh['section'=8,'tensor'=4] {'section','tensor'}, use_global_device_ids=true, to_apply=%add | all-reduce | flops 3072 | bytes 24576
  97.6 0.1 reshape.16
  97.7 0.1 reshape.17
  97.8 0.1 reshape.18
  97.8 1.4 while.19
  99.3 6.0 %fusion.14 = f32[32,8192]{1,0:T(8,128)} fusion(bf16[512,8192]{1,0:T(8,128)(2,1)} %param.7, f32[32,512]{1,0:T(8,128)S(1)} %get-tuple-element.208, f32[32]{0:T(128)S(1)} %get-tuple-element.181, f32[32]{0:T(128)S(1)} %get-tuple-element.205, s32[512]{0:T(512)S(1)} %iota_add_fusion, f32[32]{0:T(128)S(1)} %get-tuple-element.207, s32[32]{0:T(128)S(1)} %copy-done), kind=kOutput, calls=%fused_computation.20 | convolution fusion | flops 268550144 | bytes 9505280 | tf_op jit(solution)/shard_map/dot_general | solution.py:52
  105.3 0.0 all-reduce.7.cloned.1.call-update
  106.0 0.6 dynamic_slice.33
  106.6 130.1 %all-reduce.7.cloned.1.call-done = f32[32,8192]{1,0:T(8,128)} async-done(((f32[32,8192]{1,0:T(8,128)}), f32[32,8192]{1,0:T(8,128)}) %all-reduce.7.cloned.1.call-update) | async-done | bytes 1048592
  236.7 1.6 fusion.16
  (39 shorter events, 0.9 us)
Async XLA Ops:
  7.2 52.8 %copy-start = (s32[32]{0:T(128)S(1)}, s32[32]{0:T(128)}, u32[]{:S(2)}) copy-start(s32[32]{0:T(128)} %param.8) | copy-start | bytes 388
  7.2 229.5 %all-reduce.7.cloned.1.call-start = ((), (), s32[]{:S(2)}) async-start(), calls=%async_computation | async-start | bytes 2097152
Sparse Core Ops, SparseCore 0:
  105.5 131.1 all-reduce.6
where the time goes:
time: 245 us
  waiting for transfers between devices  130 us (53%)
  blocking collectives  83.4 us (34%)
  between operations  14.7 us (6%)
  matrix products  12.1 us (5%)
  other arithmetic  2.69 us (1%)
    unnamed x2, waiting for transfers between devices  130 us
    all_gather x1, blocking collectives, shards(): lax.all_gather(hidden, ('section', 'tensor'), axis=0, tiled=True)  46.4 us
    unnamed x1, blocking collectives  37 us
    dot_general x1, matrix products, shards(): lax.dot_general(lax.all_gather(hidden, ('section', 'tensor'), axis=0, til...  6.1 us
    dot_general x1, matrix products, shards(): jnp.dot(probs_grad, weight, preferred_element_type=jnp.float32)  6.03 us
  transfers between devices with their start and end apart: 1, of which 1 were waited for; matrix products, arithmetic and copies ran while one was open for 0% of the time, Pallas kernels for 0%

commit v1 on v0

v1 whole, which is shorter than its diff:
```python
import functools
import math

import jax
import jax.numpy as jnp
from jax import lax
from jax.experimental import pallas as pl
from jax.experimental.pallas import tpu as pltpu
from jax.sharding import PartitionSpec as P

AXES = ("section", "tensor")
LANES = 128
F32 = jnp.float32
BF16 = jnp.bfloat16
VMEM = pl.BlockSpec(memory_space=pltpu.VMEM)
PARAMS = pltpu.CompilerParams(vmem_limit_bytes=32 * 2**20)


def bit_groups(devices):
    bits = devices.bit_length() - 1
    groups, top = [], bits
    while top > 1:
        low = max(1, top - 2)
        groups.append((low, top - low))
        top = low
    return groups + [(0, 1)]


def swap(array, mask, devices):
    return lax.ppermute(array, AXES, [(i, i ^ mask) for i in range(devices)])


def split3(value):
    parts = []
    for _ in range(3):
        part = value.astype(BF16).astype(F32)
        parts.append(part)
        value = value - part
    return parts


def pack(values, rows):
    lane = lax.broadcasted_iota(jnp.int32, (rows, LANES), 1)
    block = jnp.zeros((rows, LANES), F32)
    for i, part in enumerate(p for v in values for p in split3(v)):
        block = jnp.where(lane == i, part, block)
    return block.astype(BF16)


def unpack(block):
    block = block.astype(F32)
    return [
        block[:, 3 * i : 3 * i + 1] + block[:, 3 * i + 1 : 3 * i + 2] + block[:, 3 * i + 2 : 3 * i + 3]
        for i in range(3)
    ]


def owner_of(row, order):
    mask, place = jnp.zeros_like(row), 0
    for low, count in order:
        mask = mask | (((row >> place) & ((1 << count) - 1)) << low)
        place += count
    return mask


def local_kernel(order, tok_dev, *refs):
    *hidden_refs, weight_ref, targets_ref, keep_ref, give_ref, acc = refs
    hidden = jnp.concatenate([ref[...] for ref in hidden_refs], 0)
    rows, depth = hidden.shape
    vocab = weight_ref.shape[0]
    me = lax.axis_index(AXES)
    logits = lax.dot_general(
        hidden, weight_ref[...], (((1,), (1,)), ((), ())), preferred_element_type=F32
    )
    tokens = targets_ref.shape[1]
    row = lax.broadcasted_iota(jnp.int32, (rows, tokens), 0)
    token = (me ^ owner_of(row // tok_dev, order)) * tok_dev + row % tok_dev
    column = lax.broadcasted_iota(jnp.int32, (rows, tokens), 1)
    target = jnp.sum(
        jnp.where(column == token, targets_ref[...], 0), axis=1, keepdims=True
    ) - me * vocab
    hit = lax.broadcasted_iota(jnp.int32, (rows, vocab), 1) == target
    largest = jnp.max(logits, axis=1, keepdims=True)
    shifted = jnp.exp(logits - largest)
    total = jnp.sum(shifted, axis=1, keepdims=True)
    at_target = jnp.sum(jnp.where(hit, logits, 0.0), axis=1, keepdims=True)
    both = jnp.concatenate([shifted.astype(BF16), hit.astype(F32).astype(BF16)], 0)
    half = rows // 2
    stats = pack((largest, total, at_target), rows)
    keep_ref[:, 2 * depth :] = stats[:half]
    give_ref[:, 2 * depth :] = stats[half:]
    step = min(depth, 1024)
    for at in range(0, depth, step):
        out = jnp.dot(both, weight_ref[:, at : at + step], preferred_element_type=F32).astype(BF16)
        keep_ref[:, at : at + step] = out[:half]
        give_ref[:, at : at + step] = out[half:rows]
        keep_ref[:, depth + at : depth + at + step] = out[rows : rows + half]
        give_ref[:, depth + at : depth + at + step] = out[rows + half :]


def merged(refs):
    stats = [unpack(ref[:, -LANES:]) for ref in refs]
    largest = functools.reduce(jnp.maximum, [s[0] for s in stats])
    scales = [jnp.exp(s[0] - largest) for s in stats]
    total = sum(a * s[1] for a, s in zip(scales, stats))
    at_target = sum(s[2] for s in stats)
    return scales, largest, total, at_target


def merge_kernel(parts, *refs):
    ins, outs = refs[:parts], refs[parts:]
    scales, *stats = merged(ins)
    rows, width = ins[0].shape
    depth = (width - LANES) // 2
    each = rows // len(outs)

    def put(at, size, value):
        for i, out in enumerate(outs):
            out[:, at : at + size] = value[i * each : (i + 1) * each]

    put(2 * depth, LANES, pack(stats, rows))
    put(0, depth, sum(a * ref[:, :depth].astype(F32) for a, ref in zip(scales, ins)).astype(BF16))
    put(depth, depth, sum(ref[:, depth : 2 * depth].astype(F32) for ref in ins).astype(BF16))


def last_kernel(parts, *refs):
    ins, (scale_ref, loss_ref, grad_ref) = refs[:parts], refs[parts:]
    scales, largest, total, at_target = merged(ins)
    width = ins[0].shape[1]
    depth = (width - LANES) // 2
    loss_ref[...] = jnp.broadcast_to(largest + jnp.log(total) - at_target, loss_ref.shape)
    summed = sum(a * ref[:, :depth].astype(F32) for a, ref in zip(scales, ins))
    hot = sum(ref[:, depth : 2 * depth].astype(F32) for ref in ins)
    grad_ref[...] = (scale_ref[...] * (summed / total - hot)).astype(BF16)


def call(kernel, ins, outs, scratch=()):
    return pl.pallas_call(
        kernel,
        out_shape=outs,
        in_specs=[VMEM] * len(ins),
        out_specs=jax.tree.map(lambda _: VMEM, outs),
        scratch_shapes=list(scratch),
        compiler_params=PARAMS,
    )(*ins)


def shards(devices, hidden, weight, targets, loss_grad):
    tok_dev, depth = hidden.shape
    groups = bit_groups(devices)
    pieces = [hidden]
    for low, count in groups:
        whole = jnp.concatenate(pieces, 0) if len(pieces) > 1 else pieces[0]
        pieces = [whole] + [swap(whole, k << low, devices) for k in range(1, 1 << count)]
    rows = devices * tok_dev
    width = 2 * depth + LANES
    half = jax.ShapeDtypeStruct((rows // 2, width), BF16)
    keep, give = call(
        functools.partial(local_kernel, groups, tok_dev),
        [*pieces, weight, targets[None, :]],
        (half, half),
        [pltpu.VMEM((8, LANES), F32)],
    )
    parts = [keep, swap(give, 1, devices)]
    for low, count in reversed(groups[:-1]):
        peers = 1 << count
        size = parts[0].shape[0] // peers
        outs = call(
            functools.partial(merge_kernel, len(parts)),
            parts,
            tuple(jax.ShapeDtypeStruct((size, width), BF16) for _ in range(peers)),
        )
        parts = [outs[0]] + [swap(outs[k], k << low, devices) for k in range(1, peers)]
    loss, grad = call(
        functools.partial(last_kernel, len(parts)),
        [*parts, loss_grad[:, None]],
        (
            jax.ShapeDtypeStruct((tok_dev, LANES), F32),
            jax.ShapeDtypeStruct((tok_dev, depth), BF16),
        ),
    )
    return loss[:, 0], grad


def solution(mesh):
    devices = math.prod(mesh.shape[axis] for axis in AXES)
    return jax.shard_map(
        functools.partial(shards, devices),
        mesh=mesh,
        in_specs=(P(AXES, None), P(AXES, None), P(), P(AXES)),
        out_specs=(P(AXES), P(AXES, None)),
        check_vma=False,
    )
```

time: 245 us -> 53.5 us (0.22)
  waiting for transfers between devices: 130 us -> 22.5 us
  blocking collectives: 83.4 us -> 0 us
  starting transfers between devices: 0.04 us -> 17.5 us
  between operations: 14.7 us -> 1.34 us
  matrix products: 12.1 us -> 0 us
  Pallas kernels: 0 us -> 5.82 us
  local copies, waits for them, and re-layouts: 1.52 us -> 5.09 us
    unnamed x2 -> x0, waiting for transfers between devices: 130 us -> none
    all_gather x1 -> x0, blocking collectives: 46.4 us -> none  [shards(): lax.all_gather(hidden, ('section', 'tensor'), axis=0, tiled=True)]
    unnamed x1 -> x0, blocking collectives: 37 us -> none
    ppermute x0 -> x14, waiting for transfers between devices: none -> 22.5 us  [swap(): return lax.ppermute(array, AXES, [(i, i ^ mask) for i in range(devices)])]
    ppermute x0 -> x14, starting transfers between devices: none -> 17.5 us  [swap(): return lax.ppermute(array, AXES, [(i, i ^ mask) for i in range(devices)])]
    dot_general x2 -> x0, matrix products: 12.1 us -> none  [the longest x1 6.1 us: shards(): lax.dot_general(lax.all_gather(hidden, ('section', 'tensor'), axis=0, til...]
    pallas_call x0 -> x4, Pallas kernels: none -> 5.82 us  [call(): pl.pallas_call(kernel, out_shape=outs, in_specs=[VMEM] * len(ins), out_sp...]
    unnamed x8 -> x4, local copies, waits for them, and re-layouts: 0.71 us -> 4.04 us
  transfers between devices with their start and end apart: 1 -> 14, of which waited for: 1 -> 11; matrix products, arithmetic and copies ran while one was open for 0% -> 0% of each run, Pallas kernels for 0% -> 0%
where the time goes in v1:
time: 53.5 us; the launch traced here: 53.1 us
  waiting for transfers between devices  22.5 us (42%)
  starting transfers between devices  17.5 us (33%)
  Pallas kernels  5.82 us (11%)
  local copies, waits for them, and re-layouts  5.09 us (10%)
  between operations  1.34 us (3%)
  other arithmetic  0.92 us (2%)
    ppermute x14, waiting for transfers between devices, swap(): return lax.ppermute(array, AXES, [(i, i ^ mask) for i in range(devices)])  22.5 us
    ppermute x14, starting transfers between devices, swap(): return lax.ppermute(array, AXES, [(i, i ^ mask) for i in range(devices)])  17.5 us
    pallas_call x4, Pallas kernels, call(): pl.pallas_call(kernel, out_shape=outs, in_specs=[VMEM] * len(ins), out_sp...  5.82 us
    unnamed x4, local copies, waits for them, and re-layouts  4.04 us
  transfers between devices with their start and end apart: 14, of which 11 were waited for; matrix products, arithmetic and copies ran while one was open for 0% of the time, Pallas kernels for 0%

profile of v1, /device:TPU:0, one launch (start us, length us, event | category | flops | bytes accessed | tf_op | source)
XLA Modules:
  0.0 53.1 jit_solution(529856721314756989)
XLA Ops:
  0.6 3.1 %collective-permute-start = (bf16[1,8192]{1,0:T(2,128)(2,1)}, bf16[1,8192]{1,0:T(2,128)(2,1)S(1)}, u32[]{:S(2)}, u32[]{:S(2)}) collective-permute-start(bf16[1,8192]{1,0:T(2,128)(2,1)} %param.4), channel_id=1, source_target_pairs={{0,8},{1,9},{2,10},{3,11},{4,12},{5,13},{6,14},{7,15},{8,0},{9,1},... | collective-permute-start | bytes 49160 | tf_op jit(solution)/shard_map/ppermute | solution.py:30
  3.7 2.6 %collective-permute-start.1 = (bf16[1,8192]{1,0:T(2,128)(2,1)}, bf16[1,8192]{1,0:T(2,128)(2,1)S(1)}, u32[]{:S(2)}, u32[]{:S(2)}) collective-permute-start(bf16[1,8192]{1,0:T(2,128)(2,1)} %param.4), channel_id=1, source_target_pairs={{0,16},{1,17},{2,18},{3,19},{4,20},{5,21},{6,22},{7,23},{8,24},{9,... | collective-permute-start | bytes 49160 | tf_op jit(solution)/shard_map/ppermute | solution.py:30
  6.3 3.0 %collective-permute-done.1 = bf16[1,8192]{1,0:T(2,128)(2,1)S(1)} collective-permute-done((bf16[1,8192]{1,0:T(2,128)(2,1)}, bf16[1,8192]{1,0:T(2,128)(2,1)S(1)}, u32[]{:S(2)}, u32[]{:S(2)}) %collective-permute-start.1) | collective-permute-done | bytes 16416 | tf_op jit(solution)/shard_map/ppermute | solution.py:30
  9.4 2.9 %collective-permute-done.2 = bf16[1,8192]{1,0:T(2,128)(2,1)S(1)} collective-permute-done((bf16[1,8192]{1,0:T(2,128)(2,1)}, bf16[1,8192]{1,0:T(2,128)(2,1)S(1)}, u32[]{:S(2)}, u32[]{:S(2)}) %collective-permute-start.2) | collective-permute-done | bytes 16416 | tf_op jit(solution)/shard_map/ppermute | solution.py:30
  12.3 0.9 %pad_maximum_fusion = bf16[4,8192]{1,0:T(4,128)(2,1)S(1)} fusion(bf16[1,8192]{1,0:T(2,128)(2,1)S(1)} %collective-permute-done.2, bf16[1,8192]{1,0:T(2,128)(2,1)S(1)} %collective-permute-done.1, bf16[1,8192]{1,0:T(2,128)(2,1)S(1)} %collective-permute-done, bf16[1,8192]{1,0:T(2,128)(2,1)} %param.4), kind=kLoop, calls=%fused_computation | loop fusion | flops 262144 | bytes 131072 | tf_op jit(solution)/shard_map/concatenate | solution.py:153
  13.2 1.6 %collective-permute-start.3 = (bf16[4,8192]{1,0:T(4,128)(2,1)S(1)}, bf16[4,8192]{1,0:T(4,128)(2,1)S(1)}, u32[]{:S(2)}, u32[]{:S(2)}) collective-permute-start(bf16[4,8192]{1,0:T(4,128)(2,1)S(1)} %pad_maximum_fusion), channel_id=1, source_target_pairs={{0,2},{1,3},{2,0},{3,1},{4,6},{5,7},{6,4},{7,5},{8,10},{9,11},{10,... | collective-permute-start | bytes 196616 | tf_op jit(solution)/shard_map/ppermute | solution.py:30
  14.8 1.5 %collective-permute-start.4 = (bf16[4,8192]{1,0:T(4,128)(2,1)S(1)}, bf16[4,8192]{1,0:T(4,128)(2,1)S(1)}, u32[]{:S(2)}, u32[]{:S(2)}) collective-permute-start(bf16[4,8192]{1,0:T(4,128)(2,1)S(1)} %pad_maximum_fusion), channel_id=1, source_target_pairs={{0,4},{1,5},{2,6},{3,7},{4,0},{5,1},{6,2},{7,3},{8,12},{9,13},{10,... | collective-permute-start | bytes 196616 | tf_op jit(solution)/shard_map/ppermute | solution.py:30
  16.7 0.8 %collective-permute-done.3 = bf16[4,8192]{1,0:T(4,128)(2,1)S(1)} collective-permute-done((bf16[4,8192]{1,0:T(4,128)(2,1)S(1)}, bf16[4,8192]{1,0:T(4,128)(2,1)S(1)}, u32[]{:S(2)}, u32[]{:S(2)}) %collective-permute-start.3) | collective-permute-done | bytes 65568 | tf_op jit(solution)/shard_map/ppermute | solution.py:30
  17.5 1.5 %collective-permute-done.4 = bf16[4,8192]{1,0:T(4,128)(2,1)S(1)} collective-permute-done((bf16[4,8192]{1,0:T(4,128)(2,1)S(1)}, bf16[4,8192]{1,0:T(4,128)(2,1)S(1)}, u32[]{:S(2)}, u32[]{:S(2)}) %collective-permute-start.4) | collective-permute-done | bytes 65568 | tf_op jit(solution)/shard_map/ppermute | solution.py:30
  19.0 2.4 %collective-permute-done.5 = bf16[4,8192]{1,0:T(4,128)(2,1)S(1)} collective-permute-done((bf16[4,8192]{1,0:T(4,128)(2,1)S(1)}, bf16[4,8192]{1,0:T(4,128)(2,1)S(1)}, u32[]{:S(2)}, u32[]{:S(2)}) %collective-permute-start.5) | collective-permute-done | bytes 65568 | tf_op jit(solution)/shard_map/ppermute | solution.py:30
  21.4 1.1 %concatenate.8.refs_0_ = bf16[16,8192]{1,0:T(8,128)(2,1)S(1)} concatenate(bf16[1,8192]{1,0:T(2,128)(2,1)} %param.4, bf16[1,8192]{1,0:T(2,128)(2,1)S(1)} %collective-permute-done, bf16[1,8192]{1,0:T(2,128)(2,1)S(1)} %collective-permute-done.1, bf16[1,8192]{1,0:T(2,128)(2,1)S(1)} %collective-permute-done.2, bf16[4,8192]{1,0:T(4,128)(2,1)S(1)} %collective-permute-done.3, ...), dimensions={0} | concatenate | bytes 524288 | tf_op jit(solution)/shard_map/concatenate | solution.py:153
  22.6 1.5 %collective-permute-done.6.refs_1_ = bf16[16,8192]{1,0:T(8,128)(2,1)S(1)} collective-permute-done((bf16[16,8192]{1,0:T(8,128)(2,1)S(1)}, bf16[16,8192]{1,0:T(8,128)(2,1)S(1)}, u32[]{:S(2)}, u32[]{:S(2)}) %collective-permute-start.6) | collective-permute-done | bytes 262176 | tf_op jit(solution)/shard_map/ppermute | solution.py:30
  24.1 3.4 %copy-done = bf16[512,8192]{1,0:T(8,128)(2,1)S(1)} copy-done((bf16[512,8192]{1,0:T(8,128)(2,1)S(1)}, bf16[512,8192]{1,0:T(8,128)(2,1)}, u32[]{:S(2)}) %copy-start) | copy-done | bytes 8388632
  28.1 4.2 %shard_map.59 = (bf16[16,16512]{1,0:T(8,128)(2,1)S(1)}, bf16[16,16512]{1,0:T(8,128)(2,1)S(1)}) custom-call(bf16[16,8192]{1,0:T(8,128)(2,1)S(1)} %concatenate.8.refs_0_, bf16[16,8192]{1,0:T(8,128)(2,1)S(1)} %collective-permute-done.6.refs_1_, bf16[512,8192]{1,0:T(8,128)(2,1)S(1)} %copy-done, s32[1,32]{1,0:T(1,128)S(1)} %bitcast.5), custom_call_target="tpu_custom_call" | custom-call | tf_op jit(solution)/shard_map/pallas_call | solution.py:138
  32.5 1.8 %collective-permute-done.7.refs_1_ = bf16[16,16512]{1,0:T(8,128)(2,1)S(1)} collective-permute-done((bf16[16,16512]{1,0:T(8,128)(2,1)S(1)}, bf16[16,16512]{1,0:T(8,128)(2,1)S(1)}, u32[]{:S(2)}, u32[]{:S(2)}) %collective-permute-start.7) | collective-permute-done | bytes 528416 | tf_op jit(solution)/shard_map/ppermute | solution.py:30
  35.3 0.8 %collective-permute-start.9 = (bf16[4,16512]{1,0:T(4,128)(2,1)S(1)}, bf16[4,16512]{1,0:T(4,128)(2,1)S(1)}, u32[]{:S(2)}, u32[]{:S(2)}) collective-permute-start(bf16[4,16512]{1,0:T(4,128)(2,1)S(1)} %get-tuple-element.18), channel_id=1, source_target_pairs={{0,4},{1,5},{2,6},{3,7},{4,0},{5,1},{6,2},{7,3},{8,12},{9,13},{10,... | collective-permute-start | bytes 396296 | tf_op jit(solution)/shard_map/ppermute | solution.py:30
  36.1 2.2 %collective-permute-start.10 = (bf16[4,16512]{1,0:T(4,128)(2,1)S(1)}, bf16[4,16512]{1,0:T(4,128)(2,1)S(1)}, u32[]{:S(2)}, u32[]{:S(2)}) collective-permute-start(bf16[4,16512]{1,0:T(4,128)(2,1)S(1)} %get-tuple-element.19), channel_id=1, source_target_pairs={{0,6},{1,7},{2,4},{3,5},{4,2},{5,3},{6,0},{7,1},{8,14},{9,15},{10,... | collective-permute-start | bytes 396296 | tf_op jit(solution)/shard_map/ppermute | solution.py:30
  38.3 2.1 %collective-permute-done.8.refs_1_ = bf16[4,16512]{1,0:T(4,128)(2,1)S(1)} collective-permute-done((bf16[4,16512]{1,0:T(4,128)(2,1)S(1)}, bf16[4,16512]{1,0:T(4,128)(2,1)S(1)}, u32[]{:S(2)}, u32[]{:S(2)}) %collective-permute-start.8) | collective-permute-done | bytes 132128 | tf_op jit(solution)/shard_map/ppermute | solution.py:30
  40.4 1.3 %collective-permute-done.9.refs_2_ = bf16[4,16512]{1,0:T(4,128)(2,1)S(1)} collective-permute-done((bf16[4,16512]{1,0:T(4,128)(2,1)S(1)}, bf16[4,16512]{1,0:T(4,128)(2,1)S(1)}, u32[]{:S(2)}, u32[]{:S(2)}) %collective-permute-start.9) | collective-permute-done | bytes 132128 | tf_op jit(solution)/shard_map/ppermute | solution.py:30
  41.7 2.7 %collective-permute-done.10.refs_3_ = bf16[4,16512]{1,0:T(4,128)(2,1)S(1)} collective-permute-done((bf16[4,16512]{1,0:T(4,128)(2,1)S(1)}, bf16[4,16512]{1,0:T(4,128)(2,1)S(1)}, u32[]{:S(2)}, u32[]{:S(2)}) %collective-permute-start.10) | collective-permute-done | bytes 132128 | tf_op jit(solution)/shard_map/ppermute | solution.py:30
  44.7 0.9 %collective-permute-start.12 = (bf16[1,16512]{1,0:T(2,128)(2,1)S(1)}, bf16[1,16512]{1,0:T(2,128)(2,1)S(1)}, u32[]{:S(2)}, u32[]{:S(2)}) collective-permute-start(bf16[1,16512]{1,0:T(2,128)(2,1)S(1)} %get-tuple-element.22), channel_id=1, source_target_pairs={{0,16},{1,17},{2,18},{3,19},{4,20},{5,21},{6,22},{7,23},{8,24},{9,... | collective-permute-start | bytes 99080 | tf_op jit(solution)/shard_map/ppermute | solution.py:30
  45.7 3.5 %collective-permute-start.13 = (bf16[1,16512]{1,0:T(2,128)(2,1)S(1)}, bf16[1,16512]{1,0:T(2,128)(2,1)S(1)}, u32[]{:S(2)}, u32[]{:S(2)}) collective-permute-start(bf16[1,16512]{1,0:T(2,128)(2,1)S(1)} %get-tuple-element.23), channel_id=1, source_target_pairs={{0,24},{1,25},{2,26},{3,27},{4,28},{5,29},{6,30},{7,31},{8,16},{9,... | collective-permute-start | bytes 99080 | tf_op jit(solution)/shard_map/ppermute | solution.py:30
  49.8 2.5 %collective-permute-done.12.refs_2_ = bf16[1,16512]{1,0:T(2,128)(2,1)S(1)} collective-permute-done((bf16[1,16512]{1,0:T(2,128)(2,1)S(1)}, bf16[1,16512]{1,0:T(2,128)(2,1)S(1)}, u32[]{:S(2)}, u32[]{:S(2)}) %collective-permute-start.12) | collective-permute-done | bytes 33056 | tf_op jit(solution)/shard_map/ppermute | solution.py:30
  52.3 0.9 %shard_map.62 = (f32[1,128]{1,0:T(1,128)}, bf16[1,8192]{1,0:T(2,128)(2,1)}) custom-call(bf16[1,16512]{1,0:T(2,128)(2,1)S(1)} %get-tuple-element.20.refs_0_, bf16[1,16512]{1,0:T(2,128)(2,1)S(1)} %collective-permute-done.11.refs_1_, bf16[1,16512]{1,0:T(2,128)(2,1)S(1)} %collective-permute-done.12.refs_2_, ...), custom_call_target="tpu_custom_call" | custom-call | tf_op jit(solution)/shard_map/pallas_call | solution.py:138
  (14 shorter events, 2.8 us)
Async XLA Ops:
  0.6 5.7 %collective-permute-start = (bf16[1,8192]{1,0:T(2,128)(2,1)}, bf16[1,8192]{1,0:T(2,128)(2,1)S(1)}, u32[]{:S(2)}, u32[]{:S(2)}) collective-permute-start(bf16[1,8192]{1,0:T(2,128)(2,1)} %param.4), channel_id=1, source_target_pairs={{0,8},{1,9},{2,10},{3,11},{4,12},{5,13},{6,14},{7,15},{8,0},{9,1},... | collective-permute-start | bytes 49160 | tf_op jit(solution)/shard_map/ppermute | solution.py:30
  3.7 5.6 %collective-permute-start.1 = (bf16[1,8192]{1,0:T(2,128)(2,1)}, bf16[1,8192]{1,0:T(2,128)(2,1)S(1)}, u32[]{:S(2)}, u32[]{:S(2)}) collective-permute-start(bf16[1,8192]{1,0:T(2,128)(2,1)} %param.4), channel_id=1, source_target_pairs={{0,16},{1,17},{2,18},{3,19},{4,20},{5,21},{6,22},{7,23},{8,24},{9,... | collective-permute-start | bytes 49160 | tf_op jit(solution)/shard_map/ppermute | solution.py:30
  6.3 5.9 %collective-permute-start.2 = (bf16[1,8192]{1,0:T(2,128)(2,1)}, bf16[1,8192]{1,0:T(2,128)(2,1)S(1)}, u32[]{:S(2)}, u32[]{:S(2)}) collective-permute-start(bf16[1,8192]{1,0:T(2,128)(2,1)} %param.4), channel_id=1, source_target_pairs={{0,24},{1,25},{2,26},{3,27},{4,28},{5,29},{6,30},{7,31},{8,16},{9,... | collective-permute-start | bytes 49160 | tf_op jit(solution)/shard_map/ppermute | solution.py:30
  13.2 4.3 %collective-permute-start.3 = (bf16[4,8192]{1,0:T(4,128)(2,1)S(1)}, bf16[4,8192]{1,0:T(4,128)(2,1)S(1)}, u32[]{:S(2)}, u32[]{:S(2)}) collective-permute-start(bf16[4,8192]{1,0:T(4,128)(2,1)S(1)} %pad_maximum_fusion), channel_id=1, source_target_pairs={{0,2},{1,3},{2,0},{3,1},{4,6},{5,7},{6,4},{7,5},{8,10},{9,11},{10,... | collective-permute-start | bytes 196616 | tf_op jit(solution)/shard_map/ppermute | solution.py:30
  14.8 4.3 %collective-permute-start.4 = (bf16[4,8192]{1,0:T(4,128)(2,1)S(1)}, bf16[4,8192]{1,0:T(4,128)(2,1)S(1)}, u32[]{:S(2)}, u32[]{:S(2)}) collective-permute-start(bf16[4,8192]{1,0:T(4,128)(2,1)S(1)} %pad_maximum_fusion), channel_id=1, source_target_pairs={{0,4},{1,5},{2,6},{3,7},{4,0},{5,1},{6,2},{7,3},{8,12},{9,13},{10,... | collective-permute-start | bytes 196616 | tf_op jit(solution)/shard_map/ppermute | solution.py:30
  16.3 5.2 %collective-permute-start.5 = (bf16[4,8192]{1,0:T(4,128)(2,1)S(1)}, bf16[4,8192]{1,0:T(4,128)(2,1)S(1)}, u32[]{:S(2)}, u32[]{:S(2)}) collective-permute-start(bf16[4,8192]{1,0:T(4,128)(2,1)S(1)} %pad_maximum_fusion), channel_id=1, source_target_pairs={{0,6},{1,7},{2,4},{3,5},{4,2},{5,3},{6,0},{7,1},{8,14},{9,15},{10,... | collective-permute-start | bytes 196616 | tf_op jit(solution)/shard_map/ppermute | solution.py:30
  22.5 1.6 %collective-permute-start.6 = (bf16[16,8192]{1,0:T(8,128)(2,1)S(1)}, bf16[16,8192]{1,0:T(8,128)(2,1)S(1)}, u32[]{:S(2)}, u32[]{:S(2)}) collective-permute-start(bf16[16,8192]{1,0:T(8,128)(2,1)S(1)} %concatenate.8.refs_0_), channel_id=1, source_target_pairs={{0,1},{1,0},{2,3},{3,2},{4,5},{5,4},{6,7},{7,6},{8,9},{9,8},{10,11... | collective-permute-start | bytes 786440 | tf_op jit(solution)/shard_map/ppermute | solution.py:30
  24.1 3.4 %copy-start = (bf16[512,8192]{1,0:T(8,128)(2,1)S(1)}, bf16[512,8192]{1,0:T(8,128)(2,1)}, u32[]{:S(2)}) copy-start(bf16[512,8192]{1,0:T(8,128)(2,1)} %refs_2_.1) | copy-start | bytes 25165828
  27.5 0.7 %copy-start.1 = (s32[32]{0:T(128)S(1)}, s32[32]{0:T(128)}, u32[]{:S(2)}) copy-start(s32[32]{0:T(128)} %param.6) | copy-start | bytes 388
  32.3 2.0 %collective-permute-start.7 = (bf16[16,16512]{1,0:T(8,128)(2,1)S(1)}, bf16[16,16512]{1,0:T(8,128)(2,1)S(1)}, u32[]{:S(2)}, u32[]{:S(2)}) collective-permute-start(bf16[16,16512]{1,0:T(8,128)(2,1)S(1)} %get-tuple-element.15), channel_id=1, source_target_pairs={{0,1},{1,0},{2,3},{3,2},{4,5},{5,4},{6,7},{7,6},{8,9},{9,8},{10,11... | collective-permute-start | bytes 1585160 | tf_op jit(solution)/shard_map/ppermute | solution.py:30
  34.7 5.6 %collective-permute-start.8 = (bf16[4,16512]{1,0:T(4,128)(2,1)S(1)}, bf16[4,16512]{1,0:T(4,128)(2,1)S(1)}, u32[]{:S(2)}, u32[]{:S(2)}) collective-permute-start(bf16[4,16512]{1,0:T(4,128)(2,1)S(1)} %get-tuple-element.17), channel_id=1, source_target_pairs={{0,2},{1,3},{2,0},{3,1},{4,6},{5,7},{6,4},{7,5},{8,10},{9,11},{10,... | collective-permute-start | bytes 396296 | tf_op jit(solution)/shard_map/ppermute | solution.py:30
  35.3 6.4 %collective-permute-start.9 = (bf16[4,16512]{1,0:T(4,128)(2,1)S(1)}, bf16[4,16512]{1,0:T(4,128)(2,1)S(1)}, u32[]{:S(2)}, u32[]{:S(2)}) collective-permute-start(bf16[4,16512]{1,0:T(4,128)(2,1)S(1)} %get-tuple-element.18), channel_id=1, source_target_pairs={{0,4},{1,5},{2,6},{3,7},{4,0},{5,1},{6,2},{7,3},{8,12},{9,13},{10,... | collective-permute-start | bytes 396296 | tf_op jit(solution)/shard_map/ppermute | solution.py:30
  36.1 8.3 %collective-permute-start.10 = (bf16[4,16512]{1,0:T(4,128)(2,1)S(1)}, bf16[4,16512]{1,0:T(4,128)(2,1)S(1)}, u32[]{:S(2)}, u32[]{:S(2)}) collective-permute-start(bf16[4,16512]{1,0:T(4,128)(2,1)S(1)} %get-tuple-element.19), channel_id=1, source_target_pairs={{0,6},{1,7},{2,4},{3,5},{4,2},{5,3},{6,0},{7,1},{8,14},{9,15},{10,... | collective-permute-start | bytes 396296 | tf_op jit(solution)/shard_map/ppermute | solution.py:30
  44.7 5.1 %collective-permute-start.11 = (bf16[1,16512]{1,0:T(2,128)(2,1)S(1)}, bf16[1,16512]{1,0:T(2,128)(2,1)S(1)}, u32[]{:S(2)}, u32[]{:S(2)}) collective-permute-start(bf16[1,16512]{1,0:T(2,128)(2,1)S(1)} %get-tuple-element.21), channel_id=1, source_target_pairs={{0,8},{1,9},{2,10},{3,11},{4,12},{5,13},{6,14},{7,15},{8,0},{9,1},... | collective-permute-start | bytes 99080 | tf_op jit(solution)/shard_map/ppermute | solution.py:30
  44.7 7.5 %collective-permute-start.12 = (bf16[1,16512]{1,0:T(2,128)(2,1)S(1)}, bf16[1,16512]{1,0:T(2,128)(2,1)S(1)}, u32[]{:S(2)}, u32[]{:S(2)}) collective-permute-start(bf16[1,16512]{1,0:T(2,128)(2,1)S(1)} %get-tuple-element.22), channel_id=1, source_target_pairs={{0,16},{1,17},{2,18},{3,19},{4,20},{5,21},{6,22},{7,23},{8,24},{9,... | collective-permute-start | bytes 99080 | tf_op jit(solution)/shard_map/ppermute | solution.py:30
  45.7 6.6 %collective-permute-start.13 = (bf16[1,16512]{1,0:T(2,128)(2,1)S(1)}, bf16[1,16512]{1,0:T(2,128)(2,1)S(1)}, u32[]{:S(2)}, u32[]{:S(2)}) collective-permute-start(bf16[1,16512]{1,0:T(2,128)(2,1)S(1)} %get-tuple-element.23), channel_id=1, source_target_pairs={{0,24},{1,25},{2,26},{3,27},{4,28},{5,29},{6,30},{7,31},{8,16},{9,... | collective-permute-start | bytes 99080 | tf_op jit(solution)/shard_map/ppermute | solution.py:30

commit v2 on v1

v2 whole, which is shorter than its diff:
```python
import functools
import math

import jax
import jax.numpy as jnp
from jax import lax
from jax.experimental import pallas as pl
from jax.experimental.pallas import tpu as pltpu
from jax.sharding import PartitionSpec as P


AXES = ("section", "tensor")
LANES = 128
F32 = jnp.float32
BF16 = jnp.bfloat16
VMEM = pl.BlockSpec(memory_space=pltpu.VMEM)
HBM = pl.BlockSpec(memory_space=pl.ANY)
SMEM = pl.BlockSpec(memory_space=pltpu.SMEM)
PARAMS = pltpu.CompilerParams(vmem_limit_bytes=32 * 2**20)
LOAD_PARAMS = pltpu.CompilerParams(vmem_limit_bytes=44 * 2**20)


def bit_groups(devices):
    bits = devices.bit_length() - 1
    groups, top = [], bits
    while top > 1:
        low = max(1, top - 2)
        groups.append((low, top - low))
        top = low
    return groups + [(0, 1)]


def swap(array, mask, devices):
    return lax.ppermute(array, AXES, [(i, i ^ mask) for i in range(devices)])


def split3(value):
    parts = []
    for _ in range(3):
        part = value.astype(BF16).astype(F32)
        parts.append(part)
        value = value - part
    return parts


def pack(values, rows):
    lane = lax.broadcasted_iota(jnp.int32, (rows, LANES), 1)
    block = jnp.zeros((rows, LANES), F32)
    for i, part in enumerate(p for v in values for p in split3(v)):
        block = jnp.where(lane == i, part, block)
    return block.astype(BF16)


def unpack(block):
    block = block.astype(F32)
    return [
        block[:, 3 * i : 3 * i + 1] + block[:, 3 * i + 1 : 3 * i + 2] + block[:, 3 * i + 2 : 3 * i + 3]
        for i in range(3)
    ]


def owner_of(row, order):
    mask, place = jnp.zeros_like(row), 0
    for low, count in order:
        mask = mask | (((row >> place) & ((1 << count) - 1)) << low)
        place += count
    return mask


def load_kernel(count, *refs):
    ins, outs, sems = refs[:count], refs[count : 2 * count], refs[2 * count]
    copies = [
        pltpu.make_async_copy(src, dst, sems.at[i]) for i, (src, dst) in enumerate(zip(ins, outs))
    ]
    for copy in copies:
        copy.start()
    for copy in copies:
        copy.wait()


def stack_kernel(*refs):
    *ins, out = refs
    out[...] = jnp.concatenate([ref[...] for ref in ins], 0)


def give_kernel(order, tok_dev, *refs):
    *hidden_refs, weight_ref, targets_ref, give_ref, probs_ref, stats_ref = refs
    hidden = jnp.concatenate([ref[...] for ref in hidden_refs], 0)
    rows, depth = hidden.shape
    vocab = weight_ref.shape[0]
    half = rows // 2
    me = lax.axis_index(AXES)
    logits = lax.dot_general(
        hidden, weight_ref[...], (((1,), (1,)), ((), ())), preferred_element_type=F32
    )
    tokens = targets_ref.shape[1]
    row = lax.broadcasted_iota(jnp.int32, (rows, tokens), 0)
    token = (me ^ owner_of(row // tok_dev, order)) * tok_dev + row % tok_dev
    column = lax.broadcasted_iota(jnp.int32, (rows, tokens), 1)
    target = jnp.sum(
        jnp.where(column == token, targets_ref[...], 0), axis=1, keepdims=True
    ) - me * vocab
    hit = lax.broadcasted_iota(jnp.int32, (rows, vocab), 1) == target
    largest = jnp.max(logits, axis=1, keepdims=True)
    shifted = jnp.exp(logits - largest)
    total = jnp.sum(shifted, axis=1, keepdims=True)
    at_target = jnp.sum(jnp.where(hit, logits, 0.0), axis=1, keepdims=True)
    shifted = shifted.astype(BF16)
    hot = hit.astype(F32).astype(BF16)
    stats = pack((largest, total, at_target), rows)
    probs_ref[:half] = shifted[:half]
    probs_ref[half:] = hot[:half]
    stats_ref[...] = stats[:half]
    give_ref[:, 2 * depth :] = stats[half:]
    both = jnp.concatenate([shifted[half:], hot[half:]], 0)
    step = min(depth, 1024)
    for at in range(0, depth, step):
        out = jnp.dot(both, weight_ref[:, at : at + step], preferred_element_type=F32).astype(BF16)
        give_ref[:, at : at + step] = out[:half]
        give_ref[:, depth + at : depth + at + step] = out[half:]


def keep_kernel(probs_ref, weight_ref, summed_ref, hot_ref):
    half, depth = summed_ref.shape
    step = min(depth, 1024)
    for at in range(0, depth, step):
        out = jnp.dot(probs_ref[...], weight_ref[:, at : at + step], preferred_element_type=F32)
        summed_ref[:, at : at + step] = out[:half]
        hot_ref[:, at : at + step] = out[half:].astype(BF16)


def views(ref):
    depth = (ref.shape[1] - LANES) // 2
    return ref.at[:, :depth], ref.at[:, depth : 2 * depth], ref.at[:, 2 * depth :]


def merged(stats_refs):
    stats = [unpack(ref[...]) for ref in stats_refs]
    largest = functools.reduce(jnp.maximum, [s[0] for s in stats])
    scales = [jnp.exp(s[0] - largest) for s in stats]
    total = sum(a * s[1] for a, s in zip(scales, stats))
    at_target = sum(s[2] for s in stats)
    return scales, largest, total, at_target


def merge(sources, outs):
    scales, *stats = merged([source[2] for source in sources])
    rows, depth = sources[0][0].shape
    each = rows // len(outs)

    def put(at, size, value):
        for i, out in enumerate(outs):
            out[:, at : at + size] = value[i * each : (i + 1) * each]

    put(2 * depth, LANES, pack(stats, rows))
    put(0, depth, sum(a * s[0][...].astype(F32) for a, s in zip(scales, sources)).astype(BF16))
    put(depth, depth, sum(s[1][...].astype(F32) for s in sources).astype(BF16))


def first_merge_kernel(summed, hot, stats, taken, *outs):
    merge([(summed, hot, stats), views(taken)], outs)


def merge_kernel(parts, *refs):
    merge([views(ref) for ref in refs[:parts]], refs[parts:])


def last_kernel(parts, *refs):
    sources, (scale_ref, loss_ref, grad_ref) = [views(ref) for ref in refs[:parts]], refs[parts:]
    scales, largest, total, at_target = merged([source[2] for source in sources])
    loss_ref[...] = jnp.broadcast_to(largest + jnp.log(total) - at_target, loss_ref.shape)
    summed = sum(a * s[0][...].astype(F32) for a, s in zip(scales, sources))
    hot = sum(s[1][...].astype(F32) for s in sources)
    sums = summed / total - hot
    for i in range(grad_ref.shape[0]):
        grad_ref[i : i + 1] = (scale_ref[i] * sums[i : i + 1]).astype(BF16)


def call(kernel, ins, outs, flops=0, specs=None, scratch=(), params=PARAMS):
    return pl.pallas_call(
        kernel,
        out_shape=outs,
        in_specs=specs or [VMEM] * len(ins),
        out_specs=jax.tree.map(lambda _: VMEM, outs),
        scratch_shapes=list(scratch),
        compiler_params=params,
        cost_estimate=pl.CostEstimate(flops=flops, bytes_accessed=flops // 64, transcendentals=0),
    )(*ins)


def shards(devices, hidden, weight, targets, loss_grad):
    return staged(devices, hidden, weight, targets[None, :], loss_grad)


def exchange(pieces, group, devices):
    got = {}
    for k in reversed(range(1, 1 << group[1])):
        got[k] = swap(pieces[k], k << group[0], devices)
    return [got[k] for k in range(1, 1 << group[1])]


def load(arrays, params):
    return call(
        functools.partial(load_kernel, len(arrays)),
        arrays,
        tuple(jax.ShapeDtypeStruct(a.shape, a.dtype) for a in arrays),
        flops=64 * sum(a.size for a in arrays),
        specs=[HBM] * len(arrays),
        params=params,
        scratch=[pltpu.SemaphoreType.DMA((len(arrays),))],
    )


def staged(devices, hidden, weight, targets, loss_grad):
    tok_dev, depth = hidden.shape
    vocab = weight.shape[0]
    groups = bit_groups(devices)
    mine, targets = load((hidden, targets), PARAMS)
    (weight,) = load((weight,), LOAD_PARAMS)
    whole, own = hidden, mine
    for i, group in enumerate(groups):
        got = exchange([whole] * (1 << group[1]), group, devices)
        if i + 1 == len(groups):
            break
        size = (1 + len(got)) * whole.shape[0]
        whole = own = call(stack_kernel, [own, *got], jax.ShapeDtypeStruct((size, depth), BF16))
    rows = devices * tok_dev
    half, width = rows // 2, 2 * depth + LANES
    flops = 4 * half * vocab * depth
    give, probs, stats = call(
        functools.partial(give_kernel, groups, tok_dev),
        [own, *got, weight, targets],
        (
            jax.ShapeDtypeStruct((half, width), BF16),
            jax.ShapeDtypeStruct((rows, vocab), BF16),
            jax.ShapeDtypeStruct((half, LANES), BF16),
        ),
        flops=3 * flops,
    )
    (taken,) = exchange([None, give], groups[-1], devices)
    summed, hot = call(
        keep_kernel,
        [probs, weight],
        (jax.ShapeDtypeStruct((half, depth), F32), jax.ShapeDtypeStruct((half, depth), BF16)),
        flops=flops,
    )
    kernel, parts = first_merge_kernel, [summed, hot, stats, taken]
    for group in reversed(groups[:-1]):
        peers = 1 << group[1]
        size = parts[0].shape[0] // peers
        outs = call(kernel, parts, (jax.ShapeDtypeStruct((size, width), BF16),) * peers)
        parts = [outs[0]] + exchange(outs, group, devices)
        kernel = functools.partial(merge_kernel, len(parts))
    loss, grad = call(
        functools.partial(last_kernel, len(parts)),
        [*parts, loss_grad],
        (
            jax.ShapeDtypeStruct((tok_dev, LANES), F32),
            jax.ShapeDtypeStruct((tok_dev, depth), BF16),
        ),
        specs=[VMEM] * len(parts) + [SMEM],
    )
    return loss[:, 0], grad


def solution(mesh):
    devices = math.prod(mesh.shape[axis] for axis in AXES)
    return jax.shard_map(
        functools.partial(shards, devices),
        mesh=mesh,
        in_specs=(P(AXES, None), P(AXES, None), P(), P(AXES)),
        out_specs=(P(AXES), P(AXES, None)),
        check_vma=False,
    )
```

time: 53.5 us -> 49.5 us (0.925)
  Pallas kernels: 5.82 us -> 11 us
  waiting for transfers between devices: 22.5 us -> 17.6 us
  local copies, waits for them, and re-layouts: 5.09 us -> 1.48 us
  other arithmetic: 0.92 us -> 0 us
    pallas_call x4 -> x9, Pallas kernels: 5.82 us -> 11 us  [call(): pl.pallas_call(kernel, out_shape=outs, in_specs=specs or [VMEM] * len(ins...]
    ppermute x14, waiting for transfers between devices: 22.5 us -> 17.6 us  [swap(): return lax.ppermute(array, AXES, [(i, i ^ mask) for i in range(devices)])]
    unnamed x4, local copies, waits for them, and re-layouts: 4.04 us -> 1.48 us
    concatenate x1 -> x0, local copies, waits for them, and re-layouts: 1.06 us -> none  [shards(): whole = jnp.concatenate(pieces, 0) if len(pieces) > 1 else pieces[0]]
    concatenate x1 -> x0, other arithmetic: 0.92 us -> none  [shards(): whole = jnp.concatenate(pieces, 0) if len(pieces) > 1 else pieces[0]]
  transfers between devices with their start and end apart: 14 -> 14, of which waited for: 11 -> 8; matrix products, arithmetic and copies ran while one was open for 0% -> 0% of each run, Pallas kernels for 0% -> 10%
where the time goes in v2:
time: 49.5 us; the launch traced here: 49.3 us
  starting transfers between devices  17.8 us (36%)
  waiting for transfers between devices  17.6 us (36%)
  Pallas kernels  11 us (22%)
  local copies, waits for them, and re-layouts  1.48 us (3%)
  between operations  1.37 us (3%)
    ppermute x14, starting transfers between devices, swap(): return lax.ppermute(array, AXES, [(i, i ^ mask) for i in range(devices)])  17.8 us
    ppermute x14, waiting for transfers between devices, swap(): return lax.ppermute(array, AXES, [(i, i ^ mask) for i in range(devices)])  17.6 us
    pallas_call x9, Pallas kernels, call(): pl.pallas_call(kernel, out_shape=outs, in_specs=specs or [VMEM] * len(ins...  11 us
    unnamed x4, local copies, waits for them, and re-layouts  1.48 us
  transfers between devices with their start and end apart: 14, of which 8 were waited for; matrix products, arithmetic and copies ran while one was open for 0% of the time, Pallas kernels for 10%

profile of v2, /device:TPU:0, one launch (start us, length us, event | category | flops | bytes accessed | tf_op | source)
XLA Modules:
  0.0 49.3 jit_solution(12568090643365923822)
XLA Ops:
  0.6 3.1 %collective-permute-start = (bf16[1,8192]{1,0:T(2,128)(2,1)}, bf16[1,8192]{1,0:T(2,128)(2,1)S(1)}, u32[]{:S(2)}, u32[]{:S(2)}) collective-permute-start(bf16[1,8192]{1,0:T(2,128)(2,1)} %refs_0_.2), channel_id=1, source_target_pairs={{0,8},{1,9},{2,10},{3,11},{4,12},{5,13},{6,14},{7,15},{8,0},{9,1},... | collective-permute-start | bytes 49160 | tf_op jit(solution)/shard_map/ppermute | solution.py:34
  3.7 2.6 %collective-permute-start.1 = (bf16[1,8192]{1,0:T(2,128)(2,1)}, bf16[1,8192]{1,0:T(2,128)(2,1)S(1)}, u32[]{:S(2)}, u32[]{:S(2)}) collective-permute-start(bf16[1,8192]{1,0:T(2,128)(2,1)} %refs_0_.2), channel_id=1, source_target_pairs={{0,16},{1,17},{2,18},{3,19},{4,20},{5,21},{6,22},{7,23},{8,24},{9,... | collective-permute-start | bytes 49160 | tf_op jit(solution)/shard_map/ppermute | solution.py:34
  6.3 0.8 %copy-done = bf16[1,8192]{1,0:T(2,128)(2,1)S(1)} copy-done((bf16[1,8192]{1,0:T(2,128)(2,1)S(1)}, bf16[1,8192]{1,0:T(2,128)(2,1)}, u32[]{:S(2)}) %copy-start) | copy-done | bytes 16408
  7.2 0.7 %copy-done.1 = s32[32]{0:T(128)S(1)} copy-done((s32[32]{0:T(128)S(1)}, s32[32]{0:T(128)}, u32[]{:S(2)}) %copy-start.1) | copy-done | bytes 152
  7.9 1.5 %collective-permute-done.1.refs_2_ = bf16[1,8192]{1,0:T(2,128)(2,1)S(1)} collective-permute-done((bf16[1,8192]{1,0:T(2,128)(2,1)}, bf16[1,8192]{1,0:T(2,128)(2,1)S(1)}, u32[]{:S(2)}, u32[]{:S(2)}) %collective-permute-start.1) | collective-permute-done | bytes 16416 | tf_op jit(solution)/shard_map/ppermute | solution.py:34
  9.4 2.9 %collective-permute-done.2.refs_3_ = bf16[1,8192]{1,0:T(2,128)(2,1)S(1)} collective-permute-done((bf16[1,8192]{1,0:T(2,128)(2,1)}, bf16[1,8192]{1,0:T(2,128)(2,1)S(1)}, u32[]{:S(2)}, u32[]{:S(2)}) %collective-permute-start.2) | collective-permute-done | bytes 16416 | tf_op jit(solution)/shard_map/ppermute | solution.py:34
  12.4 1.6 %collective-permute-start.3 = (bf16[4,8192]{1,0:T(4,128)(2,1)S(1)}, bf16[4,8192]{1,0:T(4,128)(2,1)S(1)}, u32[]{:S(2)}, u32[]{:S(2)}) collective-permute-start(bf16[4,8192]{1,0:T(4,128)(2,1)S(1)} %shard_map.60.refs_0_), channel_id=1, source_target_pairs={{0,2},{1,3},{2,0},{3,1},{4,6},{5,7},{6,4},{7,5},{8,10},{9,11},{10,... | collective-permute-start | bytes 196616 | tf_op jit(solution)/shard_map/ppermute | solution.py:34
  14.0 1.5 %collective-permute-start.4 = (bf16[4,8192]{1,0:T(4,128)(2,1)S(1)}, bf16[4,8192]{1,0:T(4,128)(2,1)S(1)}, u32[]{:S(2)}, u32[]{:S(2)}) collective-permute-start(bf16[4,8192]{1,0:T(4,128)(2,1)S(1)} %shard_map.60.refs_0_), channel_id=1, source_target_pairs={{0,4},{1,5},{2,6},{3,7},{4,0},{5,1},{6,2},{7,3},{8,12},{9,13},{10,... | collective-permute-start | bytes 196616 | tf_op jit(solution)/shard_map/ppermute | solution.py:34
  15.9 0.8 %collective-permute-done.3.refs_1_ = bf16[4,8192]{1,0:T(4,128)(2,1)S(1)} collective-permute-done((bf16[4,8192]{1,0:T(4,128)(2,1)S(1)}, bf16[4,8192]{1,0:T(4,128)(2,1)S(1)}, u32[]{:S(2)}, u32[]{:S(2)}) %collective-permute-start.3) | collective-permute-done | bytes 65568 | tf_op jit(solution)/shard_map/ppermute | solution.py:34
  16.7 1.5 %collective-permute-done.4.refs_2_ = bf16[4,8192]{1,0:T(4,128)(2,1)S(1)} collective-permute-done((bf16[4,8192]{1,0:T(4,128)(2,1)S(1)}, bf16[4,8192]{1,0:T(4,128)(2,1)S(1)}, u32[]{:S(2)}, u32[]{:S(2)}) %collective-permute-start.4) | collective-permute-done | bytes 65568 | tf_op jit(solution)/shard_map/ppermute | solution.py:34
  18.2 2.4 %collective-permute-done.5.refs_3_ = bf16[4,8192]{1,0:T(4,128)(2,1)S(1)} collective-permute-done((bf16[4,8192]{1,0:T(4,128)(2,1)S(1)}, bf16[4,8192]{1,0:T(4,128)(2,1)S(1)}, u32[]{:S(2)}, u32[]{:S(2)}) %collective-permute-start.5) | collective-permute-done | bytes 65568 | tf_op jit(solution)/shard_map/ppermute | solution.py:34
  20.8 3.4 %shard_map.62.refs_2_.weight_ref = bf16[512,8192]{1,0:T(8,128)(2,1)S(1)} custom-call(bf16[512,8192]{1,0:T(8,128)(2,1)} %refs_0_.3), custom_call_target="tpu_custom_call" | custom-call | flops 268435456 | bytes 4194304 | tf_op jit(solution)/shard_map/pallas_call | solution.py:180
  24.2 4.2 %shard_map.63 = (bf16[16,16512]{1,0:T(8,128)(2,1)S(1)}, bf16[32,512]{1,0:T(8,128)(2,1)S(1)}, bf16[16,128]{1,0:T(8,128)(2,1)S(1)}) custom-call(bf16[16,8192]{1,0:T(8,128)(2,1)S(1)} %shard_map.61.refs_0_, bf16[16,8192]{1,0:T(8,128)(2,1)S(1)} %collective-permute-done.6.refs_1_, bf16[512,8192]{1,0:T(8,128)(2,1)S(1)} %shard_map.62.refs_2_.weight_ref, ...), custom_call_target="tpu_custom_call" | custom-call | flops 805306368 | bytes 12582912 | tf_op jit(solution)/shard_map/pallas_call | solution.py:180
  28.4 0.5 %collective-permute-start.7 = (bf16[16,16512]{1,0:T(8,128)(2,1)S(1)}, bf16[16,16512]{1,0:T(8,128)(2,1)S(1)}, u32[]{:S(2)}, u32[]{:S(2)}) collective-permute-start(bf16[16,16512]{1,0:T(8,128)(2,1)S(1)} %get-tuple-element.25), channel_id=1, source_target_pairs={{0,1},{1,0},{2,3},{3,2},{4,5},{5,4},{6,7},{7,6},{8,9},{9,8},{10,11... | collective-permute-start | bytes 1585160 | tf_op jit(solution)/shard_map/ppermute | solution.py:34
  28.9 1.5 %shard_map.64 = (f32[16,8192]{1,0:T(8,128)S(1)}, bf16[16,8192]{1,0:T(8,128)(2,1)S(1)}) custom-call(bf16[32,512]{1,0:T(8,128)(2,1)S(1)} %get-tuple-element.21.probs_ref, bf16[512,8192]{1,0:T(8,128)(2,1)S(1)} %shard_map.62.refs_2_.weight_ref), custom_call_target="tpu_custom_call" | custom-call | flops 268435456 | bytes 4194304 | tf_op jit(solution)/shard_map/pallas_call | solution.py:180
  30.9 0.8 %collective-permute-start.10 = (bf16[4,16512]{1,0:T(4,128)(2,1)S(1)}, bf16[4,16512]{1,0:T(4,128)(2,1)S(1)}, u32[]{:S(2)}, u32[]{:S(2)}) collective-permute-start(bf16[4,16512]{1,0:T(4,128)(2,1)S(1)} %get-tuple-element.29), channel_id=1, source_target_pairs={{0,6},{1,7},{2,4},{3,5},{4,2},{5,3},{6,0},{7,1},{8,14},{9,15},{10,... | collective-permute-start | bytes 396296 | tf_op jit(solution)/shard_map/ppermute | solution.py:34
  31.7 1.3 %collective-permute-start.8 = (bf16[4,16512]{1,0:T(4,128)(2,1)S(1)}, bf16[4,16512]{1,0:T(4,128)(2,1)S(1)}, u32[]{:S(2)}, u32[]{:S(2)}) collective-permute-start(bf16[4,16512]{1,0:T(4,128)(2,1)S(1)} %get-tuple-element.27), channel_id=1, source_target_pairs={{0,2},{1,3},{2,0},{3,1},{4,6},{5,7},{6,4},{7,5},{8,10},{9,11},{10,... | collective-permute-start | bytes 396296 | tf_op jit(solution)/shard_map/ppermute | solution.py:34
  33.0 1.5 %collective-permute-start.9 = (bf16[4,16512]{1,0:T(4,128)(2,1)S(1)}, bf16[4,16512]{1,0:T(4,128)(2,1)S(1)}, u32[]{:S(2)}, u32[]{:S(2)}) collective-permute-start(bf16[4,16512]{1,0:T(4,128)(2,1)S(1)} %get-tuple-element.28), channel_id=1, source_target_pairs={{0,4},{1,5},{2,6},{3,7},{4,0},{5,1},{6,2},{7,3},{8,12},{9,13},{10,... | collective-permute-start | bytes 396296 | tf_op jit(solution)/shard_map/ppermute | solution.py:34
  34.5 3.8 %collective-permute-done.10.refs_3_ = bf16[4,16512]{1,0:T(4,128)(2,1)S(1)} collective-permute-done((bf16[4,16512]{1,0:T(4,128)(2,1)S(1)}, bf16[4,16512]{1,0:T(4,128)(2,1)S(1)}, u32[]{:S(2)}, u32[]{:S(2)}) %collective-permute-start.10) | collective-permute-done | bytes 132128 | tf_op jit(solution)/shard_map/ppermute | solution.py:34
  38.3 1.7 %collective-permute-done.8.refs_1_ = bf16[4,16512]{1,0:T(4,128)(2,1)S(1)} collective-permute-done((bf16[4,16512]{1,0:T(4,128)(2,1)S(1)}, bf16[4,16512]{1,0:T(4,128)(2,1)S(1)}, u32[]{:S(2)}, u32[]{:S(2)}) %collective-permute-start.8) | collective-permute-done | bytes 132128 | tf_op jit(solution)/shard_map/ppermute | solution.py:34
  40.4 0.9 %collective-permute-start.12 = (bf16[1,16512]{1,0:T(2,128)(2,1)S(1)}, bf16[1,16512]{1,0:T(2,128)(2,1)S(1)}, u32[]{:S(2)}, u32[]{:S(2)}) collective-permute-start(bf16[1,16512]{1,0:T(2,128)(2,1)S(1)} %get-tuple-element.32), channel_id=1, source_target_pairs={{0,16},{1,17},{2,18},{3,19},{4,20},{5,21},{6,22},{7,23},{8,24},{9,... | collective-permute-start | bytes 99080 | tf_op jit(solution)/shard_map/ppermute | solution.py:34
  41.3 3.5 %collective-permute-start.13 = (bf16[1,16512]{1,0:T(2,128)(2,1)S(1)}, bf16[1,16512]{1,0:T(2,128)(2,1)S(1)}, u32[]{:S(2)}, u32[]{:S(2)}) collective-permute-start(bf16[1,16512]{1,0:T(2,128)(2,1)S(1)} %get-tuple-element.33), channel_id=1, source_target_pairs={{0,24},{1,25},{2,26},{3,27},{4,28},{5,29},{6,30},{7,31},{8,16},{9,... | collective-permute-start | bytes 99080 | tf_op jit(solution)/shard_map/ppermute | solution.py:34
  45.4 3.0 %collective-permute-done.12.refs_2_ = bf16[1,16512]{1,0:T(2,128)(2,1)S(1)} collective-permute-done((bf16[1,16512]{1,0:T(2,128)(2,1)S(1)}, bf16[1,16512]{1,0:T(2,128)(2,1)S(1)}, u32[]{:S(2)}, u32[]{:S(2)}) %collective-permute-start.12) | collective-permute-done | bytes 33056 | tf_op jit(solution)/shard_map/ppermute | solution.py:34
  48.4 0.9 %shard_map.67 = (f32[1,128]{1,0:T(1,128)}, bf16[1,8192]{1,0:T(2,128)(2,1)}) custom-call(bf16[1,16512]{1,0:T(2,128)(2,1)S(1)} %get-tuple-element.30.refs_0_, bf16[1,16512]{1,0:T(2,128)(2,1)S(1)} %collective-permute-done.11.refs_1_, bf16[1,16512]{1,0:T(2,128)(2,1)S(1)} %collective-permute-done.12.refs_2_, ...), custom_call_target="tpu_custom_call" | custom-call | tf_op jit(solution)/shard_map/pallas_call | solution.py:180
  (17 shorter events, 1.6 us)
Async XLA Ops:
  0.6 7.2 %collective-permute-start = (bf16[1,8192]{1,0:T(2,128)(2,1)}, bf16[1,8192]{1,0:T(2,128)(2,1)S(1)}, u32[]{:S(2)}, u32[]{:S(2)}) collective-permute-start(bf16[1,8192]{1,0:T(2,128)(2,1)} %refs_0_.2), channel_id=1, source_target_pairs={{0,8},{1,9},{2,10},{3,11},{4,12},{5,13},{6,14},{7,15},{8,0},{9,1},... | collective-permute-start | bytes 49160 | tf_op jit(solution)/shard_map/ppermute | solution.py:34
  3.7 5.6 %collective-permute-start.1 = (bf16[1,8192]{1,0:T(2,128)(2,1)}, bf16[1,8192]{1,0:T(2,128)(2,1)S(1)}, u32[]{:S(2)}, u32[]{:S(2)}) collective-permute-start(bf16[1,8192]{1,0:T(2,128)(2,1)} %refs_0_.2), channel_id=1, source_target_pairs={{0,16},{1,17},{2,18},{3,19},{4,20},{5,21},{6,22},{7,23},{8,24},{9,... | collective-permute-start | bytes 49160 | tf_op jit(solution)/shard_map/ppermute | solution.py:34
  6.3 5.9 %collective-permute-start.2 = (bf16[1,8192]{1,0:T(2,128)(2,1)}, bf16[1,8192]{1,0:T(2,128)(2,1)S(1)}, u32[]{:S(2)}, u32[]{:S(2)}) collective-permute-start(bf16[1,8192]{1,0:T(2,128)(2,1)} %refs_0_.2), channel_id=1, source_target_pairs={{0,24},{1,25},{2,26},{3,27},{4,28},{5,29},{6,30},{7,31},{8,16},{9,... | collective-permute-start | bytes 49160 | tf_op jit(solution)/shard_map/ppermute | solution.py:34
  6.3 0.8 %copy-start = (bf16[1,8192]{1,0:T(2,128)(2,1)S(1)}, bf16[1,8192]{1,0:T(2,128)(2,1)}, u32[]{:S(2)}) copy-start(bf16[1,8192]{1,0:T(2,128)(2,1)} %refs_0_.2) | copy-start | bytes 49156
  7.2 0.7 %copy-start.1 = (s32[32]{0:T(128)S(1)}, s32[32]{0:T(128)}, u32[]{:S(2)}) copy-start(s32[32]{0:T(128)} %param.6) | copy-start | bytes 388
  12.4 4.3 %collective-permute-start.3 = (bf16[4,8192]{1,0:T(4,128)(2,1)S(1)}, bf16[4,8192]{1,0:T(4,128)(2,1)S(1)}, u32[]{:S(2)}, u32[]{:S(2)}) collective-permute-start(bf16[4,8192]{1,0:T(4,128)(2,1)S(1)} %shard_map.60.refs_0_), channel_id=1, source_target_pairs={{0,2},{1,3},{2,0},{3,1},{4,6},{5,7},{6,4},{7,5},{8,10},{9,11},{10,... | collective-permute-start | bytes 196616 | tf_op jit(solution)/shard_map/ppermute | solution.py:34
  14.0 4.3 %collective-permute-start.4 = (bf16[4,8192]{1,0:T(4,128)(2,1)S(1)}, bf16[4,8192]{1,0:T(4,128)(2,1)S(1)}, u32[]{:S(2)}, u32[]{:S(2)}) collective-permute-start(bf16[4,8192]{1,0:T(4,128)(2,1)S(1)} %shard_map.60.refs_0_), channel_id=1, source_target_pairs={{0,4},{1,5},{2,6},{3,7},{4,0},{5,1},{6,2},{7,3},{8,12},{9,13},{10,... | collective-permute-start | bytes 196616 | tf_op jit(solution)/shard_map/ppermute | solution.py:34
  15.5 5.2 %collective-permute-start.5 = (bf16[4,8192]{1,0:T(4,128)(2,1)S(1)}, bf16[4,8192]{1,0:T(4,128)(2,1)S(1)}, u32[]{:S(2)}, u32[]{:S(2)}) collective-permute-start(bf16[4,8192]{1,0:T(4,128)(2,1)S(1)} %shard_map.60.refs_0_), channel_id=1, source_target_pairs={{0,6},{1,7},{2,4},{3,5},{4,2},{5,3},{6,0},{7,1},{8,14},{9,15},{10,... | collective-permute-start | bytes 196616 | tf_op jit(solution)/shard_map/ppermute | solution.py:34
  20.7 3.5 %collective-permute-start.6 = (bf16[16,8192]{1,0:T(8,128)(2,1)S(1)}, bf16[16,8192]{1,0:T(8,128)(2,1)S(1)}, u32[]{:S(2)}, u32[]{:S(2)}) collective-permute-start(bf16[16,8192]{1,0:T(8,128)(2,1)S(1)} %shard_map.61.refs_0_), channel_id=1, source_target_pairs={{0,1},{1,0},{2,3},{3,2},{4,5},{5,4},{6,7},{7,6},{8,9},{9,8},{10,11... | collective-permute-start | bytes 786440 | tf_op jit(solution)/shard_map/ppermute | solution.py:34
  28.4 2.1 %collective-permute-start.7 = (bf16[16,16512]{1,0:T(8,128)(2,1)S(1)}, bf16[16,16512]{1,0:T(8,128)(2,1)S(1)}, u32[]{:S(2)}, u32[]{:S(2)}) collective-permute-start(bf16[16,16512]{1,0:T(8,128)(2,1)S(1)} %get-tuple-element.25), channel_id=1, source_target_pairs={{0,1},{1,0},{2,3},{3,2},{4,5},{5,4},{6,7},{7,6},{8,9},{9,8},{10,11... | collective-permute-start | bytes 1585160 | tf_op jit(solution)/shard_map/ppermute | solution.py:34
  30.9 7.4 %collective-permute-start.10 = (bf16[4,16512]{1,0:T(4,128)(2,1)S(1)}, bf16[4,16512]{1,0:T(4,128)(2,1)S(1)}, u32[]{:S(2)}, u32[]{:S(2)}) collective-permute-start(bf16[4,16512]{1,0:T(4,128)(2,1)S(1)} %get-tuple-element.29), channel_id=1, source_target_pairs={{0,6},{1,7},{2,4},{3,5},{4,2},{5,3},{6,0},{7,1},{8,14},{9,15},{10,... | collective-permute-start | bytes 396296 | tf_op jit(solution)/shard_map/ppermute | solution.py:34
  31.7 8.3 %collective-permute-start.8 = (bf16[4,16512]{1,0:T(4,128)(2,1)S(1)}, bf16[4,16512]{1,0:T(4,128)(2,1)S(1)}, u32[]{:S(2)}, u32[]{:S(2)}) collective-permute-start(bf16[4,16512]{1,0:T(4,128)(2,1)S(1)} %get-tuple-element.27), channel_id=1, source_target_pairs={{0,2},{1,3},{2,0},{3,1},{4,6},{5,7},{6,4},{7,5},{8,10},{9,11},{10,... | collective-permute-start | bytes 396296 | tf_op jit(solution)/shard_map/ppermute | solution.py:34
  33.0 7.0 %collective-permute-start.9 = (bf16[4,16512]{1,0:T(4,128)(2,1)S(1)}, bf16[4,16512]{1,0:T(4,128)(2,1)S(1)}, u32[]{:S(2)}, u32[]{:S(2)}) collective-permute-start(bf16[4,16512]{1,0:T(4,128)(2,1)S(1)} %get-tuple-element.28), channel_id=1, source_target_pairs={{0,4},{1,5},{2,6},{3,7},{4,0},{5,1},{6,2},{7,3},{8,12},{9,13},{10,... | collective-permute-start | bytes 396296 | tf_op jit(solution)/shard_map/ppermute | solution.py:34
  40.3 5.1 %collective-permute-start.11 = (bf16[1,16512]{1,0:T(2,128)(2,1)S(1)}, bf16[1,16512]{1,0:T(2,128)(2,1)S(1)}, u32[]{:S(2)}, u32[]{:S(2)}) collective-permute-start(bf16[1,16512]{1,0:T(2,128)(2,1)S(1)} %get-tuple-element.31), channel_id=1, source_target_pairs={{0,8},{1,9},{2,10},{3,11},{4,12},{5,13},{6,14},{7,15},{8,0},{9,1},... | collective-permute-start | bytes 99080 | tf_op jit(solution)/shard_map/ppermute | solution.py:34
  40.4 8.0 %collective-permute-start.12 = (bf16[1,16512]{1,0:T(2,128)(2,1)S(1)}, bf16[1,16512]{1,0:T(2,128)(2,1)S(1)}, u32[]{:S(2)}, u32[]{:S(2)}) collective-permute-start(bf16[1,16512]{1,0:T(2,128)(2,1)S(1)} %get-tuple-element.32), channel_id=1, source_target_pairs={{0,16},{1,17},{2,18},{3,19},{4,20},{5,21},{6,22},{7,23},{8,24},{9,... | collective-permute-start | bytes 99080 | tf_op jit(solution)/shard_map/ppermute | solution.py:34
  41.3 7.1 %collective-permute-start.13 = (bf16[1,16512]{1,0:T(2,128)(2,1)S(1)}, bf16[1,16512]{1,0:T(2,128)(2,1)S(1)}, u32[]{:S(2)}, u32[]{:S(2)}) collective-permute-start(bf16[1,16512]{1,0:T(2,128)(2,1)S(1)} %get-tuple-element.33), channel_id=1, source_target_pairs={{0,24},{1,25},{2,26},{3,27},{4,28},{5,29},{6,30},{7,31},{8,16},{9,... | collective-permute-start | bytes 99080 | tf_op jit(solution)/shard_map/ppermute | solution.py:34

commit v3 on v2

--- a/solution.py
+++ b/solution.py
@@ -62,7 +62,10 @@
 def owner_of(row, order):
     mask, place = jnp.zeros_like(row), 0
     for low, count in order:
-        mask = mask | (((row >> place) & ((1 << count) - 1)) << low)
+        part = (row >> place) & ((1 << count) - 1)
+        mask = mask ^ (part << low)
+        if low:
+            mask = mask ^ (part > 0).astype(jnp.int32)
         place += count
     return mask
 
@@ -195,7 +198,7 @@
 def exchange(pieces, group, devices):
     got = {}
     for k in reversed(range(1, 1 << group[1])):
-        got[k] = swap(pieces[k], k << group[0], devices)
+        got[k] = swap(pieces[k], k << group[0] | 1, devices)
     return [got[k] for k in range(1, 1 << group[1])]
 
 

time: 49.5 us -> 48.9 us (0.988); the launches traced: 49.3 us -> 48.2 us
  starting transfers between devices: 17.8 us -> 16.1 us
  waiting for transfers between devices: 17.6 us -> 18.2 us
    ppermute x14, starting transfers between devices: 17.8 us -> 16.1 us  [swap(): return lax.ppermute(array, AXES, [(i, i ^ mask) for i in range(devices)])]
    ppermute x14, waiting for transfers between devices: 17.6 us -> 18.2 us  [swap(): return lax.ppermute(array, AXES, [(i, i ^ mask) for i in range(devices)])]
  transfers between devices with their start and end apart: 14 -> 14, of which waited for: 8 -> 9; matrix products, arithmetic and copies ran while one was open for 0% -> 0% of each run, Pallas kernels for 10% -> 10%
where the time goes in v3:
time: 48.9 us; the launch traced here: 48.2 us
  waiting for transfers between devices  18.2 us (37%)
  starting transfers between devices  16.1 us (33%)
  Pallas kernels  11 us (22%)
  local copies, waits for them, and re-layouts  1.48 us (3%)
  between operations  1.35 us (3%)
    ppermute x14, waiting for transfers between devices, swap(): return lax.ppermute(array, AXES, [(i, i ^ mask) for i in range(devices)])  18.2 us
    ppermute x14, starting transfers between devices, swap(): return lax.ppermute(array, AXES, [(i, i ^ mask) for i in range(devices)])  16.1 us
    pallas_call x9, Pallas kernels, call(): pl.pallas_call(kernel, out_shape=outs, in_specs=specs or [VMEM] * len(ins...  11 us
    unnamed x4, local copies, waits for them, and re-layouts  1.48 us
  transfers between devices with their start and end apart: 14, of which 9 were waited for; matrix products, arithmetic and copies ran while one was open for 0% of the time, Pallas kernels for 10%

profile of v3, /device:TPU:0, one launch (start us, length us, event | category | flops | bytes accessed | tf_op | source)
XLA Modules:
  0.0 48.2 jit_solution(4025177448594322091)
XLA Ops:
  0.6 2.6 %collective-permute-start = (bf16[1,8192]{1,0:T(2,128)(2,1)}, bf16[1,8192]{1,0:T(2,128)(2,1)S(1)}, u32[]{:S(2)}, u32[]{:S(2)}) collective-permute-start(bf16[1,8192]{1,0:T(2,128)(2,1)} %refs_0_.2), channel_id=1, source_target_pairs={{0,9},{1,8},{2,11},{3,10},{4,13},{5,12},{6,15},{7,14},{8,1},{9,0},... | collective-permute-start | bytes 49160 | tf_op jit(solution)/shard_map/ppermute | solution.py:34
  3.2 2.9 %collective-permute-start.1 = (bf16[1,8192]{1,0:T(2,128)(2,1)}, bf16[1,8192]{1,0:T(2,128)(2,1)S(1)}, u32[]{:S(2)}, u32[]{:S(2)}) collective-permute-start(bf16[1,8192]{1,0:T(2,128)(2,1)} %refs_0_.2), channel_id=1, source_target_pairs={{0,17},{1,16},{2,19},{3,18},{4,21},{5,20},{6,23},{7,22},{8,25},{9,... | collective-permute-start | bytes 49160 | tf_op jit(solution)/shard_map/ppermute | solution.py:34
  6.1 0.8 %copy-done = bf16[1,8192]{1,0:T(2,128)(2,1)S(1)} copy-done((bf16[1,8192]{1,0:T(2,128)(2,1)S(1)}, bf16[1,8192]{1,0:T(2,128)(2,1)}, u32[]{:S(2)}) %copy-start) | copy-done | bytes 16408
  6.9 0.7 %copy-done.1 = s32[32]{0:T(128)S(1)} copy-done((s32[32]{0:T(128)S(1)}, s32[32]{0:T(128)}, u32[]{:S(2)}) %copy-start.1) | copy-done | bytes 152
  8.0 3.8 %collective-permute-done.2.refs_3_ = bf16[1,8192]{1,0:T(2,128)(2,1)S(1)} collective-permute-done((bf16[1,8192]{1,0:T(2,128)(2,1)}, bf16[1,8192]{1,0:T(2,128)(2,1)S(1)}, u32[]{:S(2)}, u32[]{:S(2)}) %collective-permute-start.2) | collective-permute-done | bytes 16416 | tf_op jit(solution)/shard_map/ppermute | solution.py:34
  11.9 1.3 %collective-permute-start.3 = (bf16[4,8192]{1,0:T(4,128)(2,1)S(1)}, bf16[4,8192]{1,0:T(4,128)(2,1)S(1)}, u32[]{:S(2)}, u32[]{:S(2)}) collective-permute-start(bf16[4,8192]{1,0:T(4,128)(2,1)S(1)} %shard_map.60.refs_0_), channel_id=1, source_target_pairs={{0,3},{1,2},{2,1},{3,0},{4,7},{5,6},{6,5},{7,4},{8,11},{9,10},{10,... | collective-permute-start | bytes 196616 | tf_op jit(solution)/shard_map/ppermute | solution.py:34
  13.2 1.5 %collective-permute-start.4 = (bf16[4,8192]{1,0:T(4,128)(2,1)S(1)}, bf16[4,8192]{1,0:T(4,128)(2,1)S(1)}, u32[]{:S(2)}, u32[]{:S(2)}) collective-permute-start(bf16[4,8192]{1,0:T(4,128)(2,1)S(1)} %shard_map.60.refs_0_), channel_id=1, source_target_pairs={{0,5},{1,4},{2,7},{3,6},{4,1},{5,0},{6,3},{7,2},{8,13},{9,12},{10,... | collective-permute-start | bytes 196616 | tf_op jit(solution)/shard_map/ppermute | solution.py:34
  14.9 1.2 %collective-permute-done.3.refs_1_ = bf16[4,8192]{1,0:T(4,128)(2,1)S(1)} collective-permute-done((bf16[4,8192]{1,0:T(4,128)(2,1)S(1)}, bf16[4,8192]{1,0:T(4,128)(2,1)S(1)}, u32[]{:S(2)}, u32[]{:S(2)}) %collective-permute-start.3) | collective-permute-done | bytes 65568 | tf_op jit(solution)/shard_map/ppermute | solution.py:34
  16.0 1.1 %collective-permute-done.4.refs_2_ = bf16[4,8192]{1,0:T(4,128)(2,1)S(1)} collective-permute-done((bf16[4,8192]{1,0:T(4,128)(2,1)S(1)}, bf16[4,8192]{1,0:T(4,128)(2,1)S(1)}, u32[]{:S(2)}, u32[]{:S(2)}) %collective-permute-start.4) | collective-permute-done | bytes 65568 | tf_op jit(solution)/shard_map/ppermute | solution.py:34
  17.1 2.5 %collective-permute-done.5.refs_3_ = bf16[4,8192]{1,0:T(4,128)(2,1)S(1)} collective-permute-done((bf16[4,8192]{1,0:T(4,128)(2,1)S(1)}, bf16[4,8192]{1,0:T(4,128)(2,1)S(1)}, u32[]{:S(2)}, u32[]{:S(2)}) %collective-permute-start.5) | collective-permute-done | bytes 65568 | tf_op jit(solution)/shard_map/ppermute | solution.py:34
  19.9 3.4 %shard_map.62.refs_2_.weight_ref = bf16[512,8192]{1,0:T(8,128)(2,1)S(1)} custom-call(bf16[512,8192]{1,0:T(8,128)(2,1)} %refs_0_.3), custom_call_target="tpu_custom_call" | custom-call | flops 268435456 | bytes 4194304 | tf_op jit(solution)/shard_map/pallas_call | solution.py:183
  23.3 4.2 %shard_map.63 = (bf16[16,16512]{1,0:T(8,128)(2,1)S(1)}, bf16[32,512]{1,0:T(8,128)(2,1)S(1)}, bf16[16,128]{1,0:T(8,128)(2,1)S(1)}) custom-call(bf16[16,8192]{1,0:T(8,128)(2,1)S(1)} %shard_map.61.refs_0_, bf16[16,8192]{1,0:T(8,128)(2,1)S(1)} %collective-permute-done.6.refs_1_, bf16[512,8192]{1,0:T(8,128)(2,1)S(1)} %shard_map.62.refs_2_.weight_ref, ...), custom_call_target="tpu_custom_call" | custom-call | flops 805306368 | bytes 12582912 | tf_op jit(solution)/shard_map/pallas_call | solution.py:183
  27.5 0.4 collective-permute-start.7
  28.0 1.5 %shard_map.64 = (f32[16,8192]{1,0:T(8,128)S(1)}, bf16[16,8192]{1,0:T(8,128)(2,1)S(1)}) custom-call(bf16[32,512]{1,0:T(8,128)(2,1)S(1)} %get-tuple-element.21.probs_ref, bf16[512,8192]{1,0:T(8,128)(2,1)S(1)} %shard_map.62.refs_2_.weight_ref), custom_call_target="tpu_custom_call" | custom-call | flops 268435456 | bytes 4194304 | tf_op jit(solution)/shard_map/pallas_call | solution.py:183
  29.5 0.4 shard_map.65
  29.9 1.2 %collective-permute-start.10 = (bf16[4,16512]{1,0:T(4,128)(2,1)S(1)}, bf16[4,16512]{1,0:T(4,128)(2,1)S(1)}, u32[]{:S(2)}, u32[]{:S(2)}) collective-permute-start(bf16[4,16512]{1,0:T(4,128)(2,1)S(1)} %get-tuple-element.29), channel_id=1, source_target_pairs={{0,7},{1,6},{2,5},{3,4},{4,3},{5,2},{6,1},{7,0},{8,15},{9,14},{10,... | collective-permute-start | bytes 396296 | tf_op jit(solution)/shard_map/ppermute | solution.py:34
  31.1 0.6 %collective-permute-start.8 = (bf16[4,16512]{1,0:T(4,128)(2,1)S(1)}, bf16[4,16512]{1,0:T(4,128)(2,1)S(1)}, u32[]{:S(2)}, u32[]{:S(2)}) collective-permute-start(bf16[4,16512]{1,0:T(4,128)(2,1)S(1)} %get-tuple-element.27), channel_id=1, source_target_pairs={{0,3},{1,2},{2,1},{3,0},{4,7},{5,6},{6,5},{7,4},{8,11},{9,10},{10,... | collective-permute-start | bytes 396296 | tf_op jit(solution)/shard_map/ppermute | solution.py:34
  31.7 1.5 %collective-permute-start.9 = (bf16[4,16512]{1,0:T(4,128)(2,1)S(1)}, bf16[4,16512]{1,0:T(4,128)(2,1)S(1)}, u32[]{:S(2)}, u32[]{:S(2)}) collective-permute-start(bf16[4,16512]{1,0:T(4,128)(2,1)S(1)} %get-tuple-element.28), channel_id=1, source_target_pairs={{0,5},{1,4},{2,7},{3,6},{4,1},{5,0},{6,3},{7,2},{8,13},{9,12},{10,... | collective-permute-start | bytes 396296 | tf_op jit(solution)/shard_map/ppermute | solution.py:34
  33.2 3.1 %collective-permute-done.10.refs_3_ = bf16[4,16512]{1,0:T(4,128)(2,1)S(1)} collective-permute-done((bf16[4,16512]{1,0:T(4,128)(2,1)S(1)}, bf16[4,16512]{1,0:T(4,128)(2,1)S(1)}, u32[]{:S(2)}, u32[]{:S(2)}) %collective-permute-start.10) | collective-permute-done | bytes 132128 | tf_op jit(solution)/shard_map/ppermute | solution.py:34
  36.3 3.2 %collective-permute-done.8.refs_1_ = bf16[4,16512]{1,0:T(4,128)(2,1)S(1)} collective-permute-done((bf16[4,16512]{1,0:T(4,128)(2,1)S(1)}, bf16[4,16512]{1,0:T(4,128)(2,1)S(1)}, u32[]{:S(2)}, u32[]{:S(2)}) %collective-permute-start.8) | collective-permute-done | bytes 132128 | tf_op jit(solution)/shard_map/ppermute | solution.py:34
  40.3 3.4 %collective-permute-start.13 = (bf16[1,16512]{1,0:T(2,128)(2,1)S(1)}, bf16[1,16512]{1,0:T(2,128)(2,1)S(1)}, u32[]{:S(2)}, u32[]{:S(2)}) collective-permute-start(bf16[1,16512]{1,0:T(2,128)(2,1)S(1)} %get-tuple-element.33), channel_id=1, source_target_pairs={{0,25},{1,24},{2,27},{3,26},{4,29},{5,28},{6,31},{7,30},{8,17},{9,... | collective-permute-start | bytes 99080 | tf_op jit(solution)/shard_map/ppermute | solution.py:34
  44.3 0.8 %collective-permute-done.11.refs_1_ = bf16[1,16512]{1,0:T(2,128)(2,1)S(1)} collective-permute-done((bf16[1,16512]{1,0:T(2,128)(2,1)S(1)}, bf16[1,16512]{1,0:T(2,128)(2,1)S(1)}, u32[]{:S(2)}, u32[]{:S(2)}) %collective-permute-start.11) | collective-permute-done | bytes 33056 | tf_op jit(solution)/shard_map/ppermute | solution.py:34
  45.1 2.2 %collective-permute-done.13.refs_3_ = bf16[1,16512]{1,0:T(2,128)(2,1)S(1)} collective-permute-done((bf16[1,16512]{1,0:T(2,128)(2,1)S(1)}, bf16[1,16512]{1,0:T(2,128)(2,1)S(1)}, u32[]{:S(2)}, u32[]{:S(2)}) %collective-permute-start.13) | collective-permute-done | bytes 33056 | tf_op jit(solution)/shard_map/ppermute | solution.py:34
  47.3 0.9 %shard_map.67 = (f32[1,128]{1,0:T(1,128)}, bf16[1,8192]{1,0:T(2,128)(2,1)}) custom-call(bf16[1,16512]{1,0:T(2,128)(2,1)S(1)} %get-tuple-element.30.refs_0_, bf16[1,16512]{1,0:T(2,128)(2,1)S(1)} %collective-permute-done.11.refs_1_, bf16[1,16512]{1,0:T(2,128)(2,1)S(1)} %collective-permute-done.12.refs_2_, ...), custom_call_target="tpu_custom_call" | custom-call | tf_op jit(solution)/shard_map/pallas_call | solution.py:183
  (17 shorter events, 1.8 us)
Async XLA Ops:
  0.6 7.0 %collective-permute-start = (bf16[1,8192]{1,0:T(2,128)(2,1)}, bf16[1,8192]{1,0:T(2,128)(2,1)S(1)}, u32[]{:S(2)}, u32[]{:S(2)}) collective-permute-start(bf16[1,8192]{1,0:T(2,128)(2,1)} %refs_0_.2), channel_id=1, source_target_pairs={{0,9},{1,8},{2,11},{3,10},{4,13},{5,12},{6,15},{7,14},{8,1},{9,0},... | collective-permute-start | bytes 49160 | tf_op jit(solution)/shard_map/ppermute | solution.py:34
  3.2 4.8 %collective-permute-start.1 = (bf16[1,8192]{1,0:T(2,128)(2,1)}, bf16[1,8192]{1,0:T(2,128)(2,1)S(1)}, u32[]{:S(2)}, u32[]{:S(2)}) collective-permute-start(bf16[1,8192]{1,0:T(2,128)(2,1)} %refs_0_.2), channel_id=1, source_target_pairs={{0,17},{1,16},{2,19},{3,18},{4,21},{5,20},{6,23},{7,22},{8,25},{9,... | collective-permute-start | bytes 49160 | tf_op jit(solution)/shard_map/ppermute | solution.py:34
  6.1 5.7 %collective-permute-start.2 = (bf16[1,8192]{1,0:T(2,128)(2,1)}, bf16[1,8192]{1,0:T(2,128)(2,1)S(1)}, u32[]{:S(2)}, u32[]{:S(2)}) collective-permute-start(bf16[1,8192]{1,0:T(2,128)(2,1)} %refs_0_.2), channel_id=1, source_target_pairs={{0,25},{1,24},{2,27},{3,26},{4,29},{5,28},{6,31},{7,30},{8,17},{9,... | collective-permute-start | bytes 49160 | tf_op jit(solution)/shard_map/ppermute | solution.py:34
  6.1 0.8 %copy-start = (bf16[1,8192]{1,0:T(2,128)(2,1)S(1)}, bf16[1,8192]{1,0:T(2,128)(2,1)}, u32[]{:S(2)}) copy-start(bf16[1,8192]{1,0:T(2,128)(2,1)} %refs_0_.2) | copy-start | bytes 49156
  6.9 0.7 %copy-start.1 = (s32[32]{0:T(128)S(1)}, s32[32]{0:T(128)}, u32[]{:S(2)}) copy-start(s32[32]{0:T(128)} %param.6) | copy-start | bytes 388
  11.9 4.2 %collective-permute-start.3 = (bf16[4,8192]{1,0:T(4,128)(2,1)S(1)}, bf16[4,8192]{1,0:T(4,128)(2,1)S(1)}, u32[]{:S(2)}, u32[]{:S(2)}) collective-permute-start(bf16[4,8192]{1,0:T(4,128)(2,1)S(1)} %shard_map.60.refs_0_), channel_id=1, source_target_pairs={{0,3},{1,2},{2,1},{3,0},{4,7},{5,6},{6,5},{7,4},{8,11},{9,10},{10,... | collective-permute-start | bytes 196616 | tf_op jit(solution)/shard_map/ppermute | solution.py:34
  13.2 4.0 %collective-permute-start.4 = (bf16[4,8192]{1,0:T(4,128)(2,1)S(1)}, bf16[4,8192]{1,0:T(4,128)(2,1)S(1)}, u32[]{:S(2)}, u32[]{:S(2)}) collective-permute-start(bf16[4,8192]{1,0:T(4,128)(2,1)S(1)} %shard_map.60.refs_0_), channel_id=1, source_target_pairs={{0,5},{1,4},{2,7},{3,6},{4,1},{5,0},{6,3},{7,2},{8,13},{9,12},{10,... | collective-permute-start | bytes 196616 | tf_op jit(solution)/shard_map/ppermute | solution.py:34
  14.7 5.0 %collective-permute-start.5 = (bf16[4,8192]{1,0:T(4,128)(2,1)S(1)}, bf16[4,8192]{1,0:T(4,128)(2,1)S(1)}, u32[]{:S(2)}, u32[]{:S(2)}) collective-permute-start(bf16[4,8192]{1,0:T(4,128)(2,1)S(1)} %shard_map.60.refs_0_), channel_id=1, source_target_pairs={{0,7},{1,6},{2,5},{3,4},{4,3},{5,2},{6,1},{7,0},{8,15},{9,14},{10,... | collective-permute-start | bytes 196616 | tf_op jit(solution)/shard_map/ppermute | solution.py:34
  19.7 3.6 %collective-permute-start.6 = (bf16[16,8192]{1,0:T(8,128)(2,1)S(1)}, bf16[16,8192]{1,0:T(8,128)(2,1)S(1)}, u32[]{:S(2)}, u32[]{:S(2)}) collective-permute-start(bf16[16,8192]{1,0:T(8,128)(2,1)S(1)} %shard_map.61.refs_0_), channel_id=1, source_target_pairs={{0,1},{1,0},{2,3},{3,2},{4,5},{5,4},{6,7},{7,6},{8,9},{9,8},{10,11... | collective-permute-start | bytes 786440 | tf_op jit(solution)/shard_map/ppermute | solution.py:34
  27.5 2.0 %collective-permute-start.7 = (bf16[16,16512]{1,0:T(8,128)(2,1)S(1)}, bf16[16,16512]{1,0:T(8,128)(2,1)S(1)}, u32[]{:S(2)}, u32[]{:S(2)}) collective-permute-start(bf16[16,16512]{1,0:T(8,128)(2,1)S(1)} %get-tuple-element.25), channel_id=1, source_target_pairs={{0,1},{1,0},{2,3},{3,2},{4,5},{5,4},{6,7},{7,6},{8,9},{9,8},{10,11... | collective-permute-start | bytes 1585160 | tf_op jit(solution)/shard_map/ppermute | solution.py:34
  29.9 6.3 %collective-permute-start.10 = (bf16[4,16512]{1,0:T(4,128)(2,1)S(1)}, bf16[4,16512]{1,0:T(4,128)(2,1)S(1)}, u32[]{:S(2)}, u32[]{:S(2)}) collective-permute-start(bf16[4,16512]{1,0:T(4,128)(2,1)S(1)} %get-tuple-element.29), channel_id=1, source_target_pairs={{0,7},{1,6},{2,5},{3,4},{4,3},{5,2},{6,1},{7,0},{8,15},{9,14},{10,... | collective-permute-start | bytes 396296 | tf_op jit(solution)/shard_map/ppermute | solution.py:34
  31.1 8.4 %collective-permute-start.8 = (bf16[4,16512]{1,0:T(4,128)(2,1)S(1)}, bf16[4,16512]{1,0:T(4,128)(2,1)S(1)}, u32[]{:S(2)}, u32[]{:S(2)}) collective-permute-start(bf16[4,16512]{1,0:T(4,128)(2,1)S(1)} %get-tuple-element.27), channel_id=1, source_target_pairs={{0,3},{1,2},{2,1},{3,0},{4,7},{5,6},{6,5},{7,4},{8,11},{9,10},{10,... | collective-permute-start | bytes 396296 | tf_op jit(solution)/shard_map/ppermute | solution.py:34
  31.7 7.8 %collective-permute-start.9 = (bf16[4,16512]{1,0:T(4,128)(2,1)S(1)}, bf16[4,16512]{1,0:T(4,128)(2,1)S(1)}, u32[]{:S(2)}, u32[]{:S(2)}) collective-permute-start(bf16[4,16512]{1,0:T(4,128)(2,1)S(1)} %get-tuple-element.28), channel_id=1, source_target_pairs={{0,5},{1,4},{2,7},{3,6},{4,1},{5,0},{6,3},{7,2},{8,13},{9,12},{10,... | collective-permute-start | bytes 396296 | tf_op jit(solution)/shard_map/ppermute | solution.py:34
  39.8 5.3 %collective-permute-start.11 = (bf16[1,16512]{1,0:T(2,128)(2,1)S(1)}, bf16[1,16512]{1,0:T(2,128)(2,1)S(1)}, u32[]{:S(2)}, u32[]{:S(2)}) collective-permute-start(bf16[1,16512]{1,0:T(2,128)(2,1)S(1)} %get-tuple-element.31), channel_id=1, source_target_pairs={{0,9},{1,8},{2,11},{3,10},{4,13},{5,12},{6,15},{7,14},{8,1},{9,0},... | collective-permute-start | bytes 99080 | tf_op jit(solution)/shard_map/ppermute | solution.py:34
  39.9 5.2 %collective-permute-start.12 = (bf16[1,16512]{1,0:T(2,128)(2,1)S(1)}, bf16[1,16512]{1,0:T(2,128)(2,1)S(1)}, u32[]{:S(2)}, u32[]{:S(2)}) collective-permute-start(bf16[1,16512]{1,0:T(2,128)(2,1)S(1)} %get-tuple-element.32), channel_id=1, source_target_pairs={{0,17},{1,16},{2,19},{3,18},{4,21},{5,20},{6,23},{7,22},{8,25},{9,... | collective-permute-start | bytes 99080 | tf_op jit(solution)/shard_map/ppermute | solution.py:34
  40.3 7.0 %collective-permute-start.13 = (bf16[1,16512]{1,0:T(2,128)(2,1)S(1)}, bf16[1,16512]{1,0:T(2,128)(2,1)S(1)}, u32[]{:S(2)}, u32[]{:S(2)}) collective-permute-start(bf16[1,16512]{1,0:T(2,128)(2,1)S(1)} %get-tuple-element.33), channel_id=1, source_target_pairs={{0,25},{1,24},{2,27},{3,26},{4,29},{5,28},{6,31},{7,30},{8,17},{9,... | collective-permute-start | bytes 99080 | tf_op jit(solution)/shard_map/ppermute | solution.py:34

commit v4 on v3

--- a/solution.py
+++ b/solution.py
@@ -11,6 +11,7 @@
 
 AXES = ("section", "tensor")
 LANES = 128
+PIECES = 4
 F32 = jnp.float32
 BF16 = jnp.bfloat16
 VMEM = pl.BlockSpec(memory_space=pltpu.VMEM)
@@ -72,9 +73,13 @@
 
 def load_kernel(count, *refs):
     ins, outs, sems = refs[:count], refs[count : 2 * count], refs[2 * count]
-    copies = [
-        pltpu.make_async_copy(src, dst, sems.at[i]) for i, (src, dst) in enumerate(zip(ins, outs))
-    ]
+    copies = []
+    for i, (src, dst) in enumerate(zip(ins, outs)):
+        rows = src.shape[0]
+        cuts = PIECES if rows % (8 * PIECES) == 0 else 1
+        for k in range(cuts):
+            part = pl.ds(k * (rows // cuts), rows // cuts)
+            copies.append(pltpu.make_async_copy(src.at[part], dst.at[part], sems.at[i * PIECES + k]))
     for copy in copies:
         copy.start()
     for copy in copies:
@@ -210,7 +215,7 @@
         flops=64 * sum(a.size for a in arrays),
         specs=[HBM] * len(arrays),
         params=params,
-        scratch=[pltpu.SemaphoreType.DMA((len(arrays),))],
+        scratch=[pltpu.SemaphoreType.DMA((len(arrays) * PIECES,))],
     )
 
 

time: 48.9 us -> 48.9 us (level)
  transfers between devices with their start and end apart: 14 -> 14, of which waited for: 9 -> 9; matrix products, arithmetic and copies ran while one was open for 0% -> 0% of each run, Pallas kernels for 10% -> 11%
where the time goes in v4:
time: 48.9 us; the launch traced here: 48.3 us
  waiting for transfers between devices  18.2 us (37%)
  starting transfers between devices  16.1 us (33%)
  Pallas kernels  11.1 us (23%)
  local copies, waits for them, and re-layouts  1.48 us (3%)
  between operations  1.35 us (3%)
    ppermute x14, waiting for transfers between devices, swap(): return lax.ppermute(array, AXES, [(i, i ^ mask) for i in range(devices)])  18.2 us
    ppermute x14, starting transfers between devices, swap(): return lax.ppermute(array, AXES, [(i, i ^ mask) for i in range(devices)])  16.1 us
    pallas_call x9, Pallas kernels, call(): pl.pallas_call(kernel, out_shape=outs, in_specs=specs or [VMEM] * len(ins...  11.1 us
    unnamed x4, local copies, waits for them, and re-layouts  1.48 us
  transfers between devices with their start and end apart: 14, of which 9 were waited for; matrix products, arithmetic and copies ran while one was open for 0% of the time, Pallas kernels for 11%

profile of v4, /device:TPU:0, one launch (start us, length us, event | category | flops | bytes accessed | tf_op | source)
XLA Modules:
  0.0 48.3 jit_solution(13483653131584784360)
XLA Ops:
  0.6 2.6 %collective-permute-start = (bf16[1,8192]{1,0:T(2,128)(2,1)}, bf16[1,8192]{1,0:T(2,128)(2,1)S(1)}, u32[]{:S(2)}, u32[]{:S(2)}) collective-permute-start(bf16[1,8192]{1,0:T(2,128)(2,1)} %refs_0_.2), channel_id=1, source_target_pairs={{0,9},{1,8},{2,11},{3,10},{4,13},{5,12},{6,15},{7,14},{8,1},{9,0},... | collective-permute-start | bytes 49160 | tf_op jit(solution)/shard_map/ppermute | solution.py:35
  3.2 2.9 %collective-permute-start.1 = (bf16[1,8192]{1,0:T(2,128)(2,1)}, bf16[1,8192]{1,0:T(2,128)(2,1)S(1)}, u32[]{:S(2)}, u32[]{:S(2)}) collective-permute-start(bf16[1,8192]{1,0:T(2,128)(2,1)} %refs_0_.2), channel_id=1, source_target_pairs={{0,17},{1,16},{2,19},{3,18},{4,21},{5,20},{6,23},{7,22},{8,25},{9,... | collective-permute-start | bytes 49160 | tf_op jit(solution)/shard_map/ppermute | solution.py:35
  6.1 0.8 %copy-done = bf16[1,8192]{1,0:T(2,128)(2,1)S(1)} copy-done((bf16[1,8192]{1,0:T(2,128)(2,1)S(1)}, bf16[1,8192]{1,0:T(2,128)(2,1)}, u32[]{:S(2)}) %copy-start) | copy-done | bytes 16408
  6.9 0.7 %copy-done.1 = s32[32]{0:T(128)S(1)} copy-done((s32[32]{0:T(128)S(1)}, s32[32]{0:T(128)}, u32[]{:S(2)}) %copy-start.1) | copy-done | bytes 152
  8.0 3.8 %collective-permute-done.2.refs_3_ = bf16[1,8192]{1,0:T(2,128)(2,1)S(1)} collective-permute-done((bf16[1,8192]{1,0:T(2,128)(2,1)}, bf16[1,8192]{1,0:T(2,128)(2,1)S(1)}, u32[]{:S(2)}, u32[]{:S(2)}) %collective-permute-start.2) | collective-permute-done | bytes 16416 | tf_op jit(solution)/shard_map/ppermute | solution.py:35
  11.9 1.3 %collective-permute-start.3 = (bf16[4,8192]{1,0:T(4,128)(2,1)S(1)}, bf16[4,8192]{1,0:T(4,128)(2,1)S(1)}, u32[]{:S(2)}, u32[]{:S(2)}) collective-permute-start(bf16[4,8192]{1,0:T(4,128)(2,1)S(1)} %shard_map.60.refs_0_), channel_id=1, source_target_pairs={{0,3},{1,2},{2,1},{3,0},{4,7},{5,6},{6,5},{7,4},{8,11},{9,10},{10,... | collective-permute-start | bytes 196616 | tf_op jit(solution)/shard_map/ppermute | solution.py:35
  13.2 1.5 %collective-permute-start.4 = (bf16[4,8192]{1,0:T(4,128)(2,1)S(1)}, bf16[4,8192]{1,0:T(4,128)(2,1)S(1)}, u32[]{:S(2)}, u32[]{:S(2)}) collective-permute-start(bf16[4,8192]{1,0:T(4,128)(2,1)S(1)} %shard_map.60.refs_0_), channel_id=1, source_target_pairs={{0,5},{1,4},{2,7},{3,6},{4,1},{5,0},{6,3},{7,2},{8,13},{9,12},{10,... | collective-permute-start | bytes 196616 | tf_op jit(solution)/shard_map/ppermute | solution.py:35
  14.9 1.2 %collective-permute-done.3.refs_1_ = bf16[4,8192]{1,0:T(4,128)(2,1)S(1)} collective-permute-done((bf16[4,8192]{1,0:T(4,128)(2,1)S(1)}, bf16[4,8192]{1,0:T(4,128)(2,1)S(1)}, u32[]{:S(2)}, u32[]{:S(2)}) %collective-permute-start.3) | collective-permute-done | bytes 65568 | tf_op jit(solution)/shard_map/ppermute | solution.py:35
  16.0 1.1 %collective-permute-done.4.refs_2_ = bf16[4,8192]{1,0:T(4,128)(2,1)S(1)} collective-permute-done((bf16[4,8192]{1,0:T(4,128)(2,1)S(1)}, bf16[4,8192]{1,0:T(4,128)(2,1)S(1)}, u32[]{:S(2)}, u32[]{:S(2)}) %collective-permute-start.4) | collective-permute-done | bytes 65568 | tf_op jit(solution)/shard_map/ppermute | solution.py:35
  17.1 2.5 %collective-permute-done.5.refs_3_ = bf16[4,8192]{1,0:T(4,128)(2,1)S(1)} collective-permute-done((bf16[4,8192]{1,0:T(4,128)(2,1)S(1)}, bf16[4,8192]{1,0:T(4,128)(2,1)S(1)}, u32[]{:S(2)}, u32[]{:S(2)}) %collective-permute-start.5) | collective-permute-done | bytes 65568 | tf_op jit(solution)/shard_map/ppermute | solution.py:35
  19.9 3.5 %shard_map.62.refs_2_.weight_ref = bf16[512,8192]{1,0:T(8,128)(2,1)S(1)} custom-call(bf16[512,8192]{1,0:T(8,128)(2,1)} %refs_0_.3), custom_call_target="tpu_custom_call" | custom-call | flops 268435456 | bytes 4194304 | tf_op jit(solution)/shard_map/pallas_call | solution.py:188
  23.4 4.2 %shard_map.63 = (bf16[16,16512]{1,0:T(8,128)(2,1)S(1)}, bf16[32,512]{1,0:T(8,128)(2,1)S(1)}, bf16[16,128]{1,0:T(8,128)(2,1)S(1)}) custom-call(bf16[16,8192]{1,0:T(8,128)(2,1)S(1)} %shard_map.61.refs_0_, bf16[16,8192]{1,0:T(8,128)(2,1)S(1)} %collective-permute-done.6.refs_1_, bf16[512,8192]{1,0:T(8,128)(2,1)S(1)} %shard_map.62.refs_2_.weight_ref, ...), custom_call_target="tpu_custom_call" | custom-call | flops 805306368 | bytes 12582912 | tf_op jit(solution)/shard_map/pallas_call | solution.py:188
  27.6 0.4 collective-permute-start.7
  28.1 1.5 %shard_map.64 = (f32[16,8192]{1,0:T(8,128)S(1)}, bf16[16,8192]{1,0:T(8,128)(2,1)S(1)}) custom-call(bf16[32,512]{1,0:T(8,128)(2,1)S(1)} %get-tuple-element.21.probs_ref, bf16[512,8192]{1,0:T(8,128)(2,1)S(1)} %shard_map.62.refs_2_.weight_ref), custom_call_target="tpu_custom_call" | custom-call | flops 268435456 | bytes 4194304 | tf_op jit(solution)/shard_map/pallas_call | solution.py:188
  29.6 0.4 shard_map.65
  30.0 1.2 %collective-permute-start.10 = (bf16[4,16512]{1,0:T(4,128)(2,1)S(1)}, bf16[4,16512]{1,0:T(4,128)(2,1)S(1)}, u32[]{:S(2)}, u32[]{:S(2)}) collective-permute-start(bf16[4,16512]{1,0:T(4,128)(2,1)S(1)} %get-tuple-element.29), channel_id=1, source_target_pairs={{0,7},{1,6},{2,5},{3,4},{4,3},{5,2},{6,1},{7,0},{8,15},{9,14},{10,... | collective-permute-start | bytes 396296 | tf_op jit(solution)/shard_map/ppermute | solution.py:35
  31.2 0.6 %collective-permute-start.8 = (bf16[4,16512]{1,0:T(4,128)(2,1)S(1)}, bf16[4,16512]{1,0:T(4,128)(2,1)S(1)}, u32[]{:S(2)}, u32[]{:S(2)}) collective-permute-start(bf16[4,16512]{1,0:T(4,128)(2,1)S(1)} %get-tuple-element.27), channel_id=1, source_target_pairs={{0,3},{1,2},{2,1},{3,0},{4,7},{5,6},{6,5},{7,4},{8,11},{9,10},{10,... | collective-permute-start | bytes 396296 | tf_op jit(solution)/shard_map/ppermute | solution.py:35
  31.8 1.5 %collective-permute-start.9 = (bf16[4,16512]{1,0:T(4,128)(2,1)S(1)}, bf16[4,16512]{1,0:T(4,128)(2,1)S(1)}, u32[]{:S(2)}, u32[]{:S(2)}) collective-permute-start(bf16[4,16512]{1,0:T(4,128)(2,1)S(1)} %get-tuple-element.28), channel_id=1, source_target_pairs={{0,5},{1,4},{2,7},{3,6},{4,1},{5,0},{6,3},{7,2},{8,13},{9,12},{10,... | collective-permute-start | bytes 396296 | tf_op jit(solution)/shard_map/ppermute | solution.py:35
  33.3 3.1 %collective-permute-done.10.refs_3_ = bf16[4,16512]{1,0:T(4,128)(2,1)S(1)} collective-permute-done((bf16[4,16512]{1,0:T(4,128)(2,1)S(1)}, bf16[4,16512]{1,0:T(4,128)(2,1)S(1)}, u32[]{:S(2)}, u32[]{:S(2)}) %collective-permute-start.10) | collective-permute-done | bytes 132128 | tf_op jit(solution)/shard_map/ppermute | solution.py:35
  36.4 3.2 %collective-permute-done.8.refs_1_ = bf16[4,16512]{1,0:T(4,128)(2,1)S(1)} collective-permute-done((bf16[4,16512]{1,0:T(4,128)(2,1)S(1)}, bf16[4,16512]{1,0:T(4,128)(2,1)S(1)}, u32[]{:S(2)}, u32[]{:S(2)}) %collective-permute-start.8) | collective-permute-done | bytes 132128 | tf_op jit(solution)/shard_map/ppermute | solution.py:35
  40.4 3.4 %collective-permute-start.13 = (bf16[1,16512]{1,0:T(2,128)(2,1)S(1)}, bf16[1,16512]{1,0:T(2,128)(2,1)S(1)}, u32[]{:S(2)}, u32[]{:S(2)}) collective-permute-start(bf16[1,16512]{1,0:T(2,128)(2,1)S(1)} %get-tuple-element.33), channel_id=1, source_target_pairs={{0,25},{1,24},{2,27},{3,26},{4,29},{5,28},{6,31},{7,30},{8,17},{9,... | collective-permute-start | bytes 99080 | tf_op jit(solution)/shard_map/ppermute | solution.py:35
  44.4 0.8 %collective-permute-done.11.refs_1_ = bf16[1,16512]{1,0:T(2,128)(2,1)S(1)} collective-permute-done((bf16[1,16512]{1,0:T(2,128)(2,1)S(1)}, bf16[1,16512]{1,0:T(2,128)(2,1)S(1)}, u32[]{:S(2)}, u32[]{:S(2)}) %collective-permute-start.11) | collective-permute-done | bytes 33056 | tf_op jit(solution)/shard_map/ppermute | solution.py:35
  45.2 2.2 %collective-permute-done.13.refs_3_ = bf16[1,16512]{1,0:T(2,128)(2,1)S(1)} collective-permute-done((bf16[1,16512]{1,0:T(2,128)(2,1)S(1)}, bf16[1,16512]{1,0:T(2,128)(2,1)S(1)}, u32[]{:S(2)}, u32[]{:S(2)}) %collective-permute-start.13) | collective-permute-done | bytes 33056 | tf_op jit(solution)/shard_map/ppermute | solution.py:35
  47.4 0.9 %shard_map.67 = (f32[1,128]{1,0:T(1,128)}, bf16[1,8192]{1,0:T(2,128)(2,1)}) custom-call(bf16[1,16512]{1,0:T(2,128)(2,1)S(1)} %get-tuple-element.30.refs_0_, bf16[1,16512]{1,0:T(2,128)(2,1)S(1)} %collective-permute-done.11.refs_1_, bf16[1,16512]{1,0:T(2,128)(2,1)S(1)} %collective-permute-done.12.refs_2_, ...), custom_call_target="tpu_custom_call" | custom-call | tf_op jit(solution)/shard_map/pallas_call | solution.py:188
  (17 shorter events, 1.8 us)
Async XLA Ops:
  0.6 7.0 %collective-permute-start = (bf16[1,8192]{1,0:T(2,128)(2,1)}, bf16[1,8192]{1,0:T(2,128)(2,1)S(1)}, u32[]{:S(2)}, u32[]{:S(2)}) collective-permute-start(bf16[1,8192]{1,0:T(2,128)(2,1)} %refs_0_.2), channel_id=1, source_target_pairs={{0,9},{1,8},{2,11},{3,10},{4,13},{5,12},{6,15},{7,14},{8,1},{9,0},... | collective-permute-start | bytes 49160 | tf_op jit(solution)/shard_map/ppermute | solution.py:35
  3.2 4.8 %collective-permute-start.1 = (bf16[1,8192]{1,0:T(2,128)(2,1)}, bf16[1,8192]{1,0:T(2,128)(2,1)S(1)}, u32[]{:S(2)}, u32[]{:S(2)}) collective-permute-start(bf16[1,8192]{1,0:T(2,128)(2,1)} %refs_0_.2), channel_id=1, source_target_pairs={{0,17},{1,16},{2,19},{3,18},{4,21},{5,20},{6,23},{7,22},{8,25},{9,... | collective-permute-start | bytes 49160 | tf_op jit(solution)/shard_map/ppermute | solution.py:35
  6.1 5.7 %collective-permute-start.2 = (bf16[1,8192]{1,0:T(2,128)(2,1)}, bf16[1,8192]{1,0:T(2,128)(2,1)S(1)}, u32[]{:S(2)}, u32[]{:S(2)}) collective-permute-start(bf16[1,8192]{1,0:T(2,128)(2,1)} %refs_0_.2), channel_id=1, source_target_pairs={{0,25},{1,24},{2,27},{3,26},{4,29},{5,28},{6,31},{7,30},{8,17},{9,... | collective-permute-start | bytes 49160 | tf_op jit(solution)/shard_map/ppermute | solution.py:35
  6.1 0.8 %copy-start = (bf16[1,8192]{1,0:T(2,128)(2,1)S(1)}, bf16[1,8192]{1,0:T(2,128)(2,1)}, u32[]{:S(2)}) copy-start(bf16[1,8192]{1,0:T(2,128)(2,1)} %refs_0_.2) | copy-start | bytes 49156
  6.9 0.7 %copy-start.1 = (s32[32]{0:T(128)S(1)}, s32[32]{0:T(128)}, u32[]{:S(2)}) copy-start(s32[32]{0:T(128)} %param.6) | copy-start | bytes 388
  11.9 4.2 %collective-permute-start.3 = (bf16[4,8192]{1,0:T(4,128)(2,1)S(1)}, bf16[4,8192]{1,0:T(4,128)(2,1)S(1)}, u32[]{:S(2)}, u32[]{:S(2)}) collective-permute-start(bf16[4,8192]{1,0:T(4,128)(2,1)S(1)} %shard_map.60.refs_0_), channel_id=1, source_target_pairs={{0,3},{1,2},{2,1},{3,0},{4,7},{5,6},{6,5},{7,4},{8,11},{9,10},{10,... | collective-permute-start | bytes 196616 | tf_op jit(solution)/shard_map/ppermute | solution.py:35
  13.2 4.0 %collective-permute-start.4 = (bf16[4,8192]{1,0:T(4,128)(2,1)S(1)}, bf16[4,8192]{1,0:T(4,128)(2,1)S(1)}, u32[]{:S(2)}, u32[]{:S(2)}) collective-permute-start(bf16[4,8192]{1,0:T(4,128)(2,1)S(1)} %shard_map.60.refs_0_), channel_id=1, source_target_pairs={{0,5},{1,4},{2,7},{3,6},{4,1},{5,0},{6,3},{7,2},{8,13},{9,12},{10,... | collective-permute-start | bytes 196616 | tf_op jit(solution)/shard_map/ppermute | solution.py:35
  14.7 5.0 %collective-permute-start.5 = (bf16[4,8192]{1,0:T(4,128)(2,1)S(1)}, bf16[4,8192]{1,0:T(4,128)(2,1)S(1)}, u32[]{:S(2)}, u32[]{:S(2)}) collective-permute-start(bf16[4,8192]{1,0:T(4,128)(2,1)S(1)} %shard_map.60.refs_0_), channel_id=1, source_target_pairs={{0,7},{1,6},{2,5},{3,4},{4,3},{5,2},{6,1},{7,0},{8,15},{9,14},{10,... | collective-permute-start | bytes 196616 | tf_op jit(solution)/shard_map/ppermute | solution.py:35
  19.7 3.7 %collective-permute-start.6 = (bf16[16,8192]{1,0:T(8,128)(2,1)S(1)}, bf16[16,8192]{1,0:T(8,128)(2,1)S(1)}, u32[]{:S(2)}, u32[]{:S(2)}) collective-permute-start(bf16[16,8192]{1,0:T(8,128)(2,1)S(1)} %shard_map.61.refs_0_), channel_id=1, source_target_pairs={{0,1},{1,0},{2,3},{3,2},{4,5},{5,4},{6,7},{7,6},{8,9},{9,8},{10,11... | collective-permute-start | bytes 786440 | tf_op jit(solution)/shard_map/ppermute | solution.py:35
  27.6 2.0 %collective-permute-start.7 = (bf16[16,16512]{1,0:T(8,128)(2,1)S(1)}, bf16[16,16512]{1,0:T(8,128)(2,1)S(1)}, u32[]{:S(2)}, u32[]{:S(2)}) collective-permute-start(bf16[16,16512]{1,0:T(8,128)(2,1)S(1)} %get-tuple-element.25), channel_id=1, source_target_pairs={{0,1},{1,0},{2,3},{3,2},{4,5},{5,4},{6,7},{7,6},{8,9},{9,8},{10,11... | collective-permute-start | bytes 1585160 | tf_op jit(solution)/shard_map/ppermute | solution.py:35
  30.0 6.3 %collective-permute-start.10 = (bf16[4,16512]{1,0:T(4,128)(2,1)S(1)}, bf16[4,16512]{1,0:T(4,128)(2,1)S(1)}, u32[]{:S(2)}, u32[]{:S(2)}) collective-permute-start(bf16[4,16512]{1,0:T(4,128)(2,1)S(1)} %get-tuple-element.29), channel_id=1, source_target_pairs={{0,7},{1,6},{2,5},{3,4},{4,3},{5,2},{6,1},{7,0},{8,15},{9,14},{10,... | collective-permute-start | bytes 396296 | tf_op jit(solution)/shard_map/ppermute | solution.py:35
  31.2 8.4 %collective-permute-start.8 = (bf16[4,16512]{1,0:T(4,128)(2,1)S(1)}, bf16[4,16512]{1,0:T(4,128)(2,1)S(1)}, u32[]{:S(2)}, u32[]{:S(2)}) collective-permute-start(bf16[4,16512]{1,0:T(4,128)(2,1)S(1)} %get-tuple-element.27), channel_id=1, source_target_pairs={{0,3},{1,2},{2,1},{3,0},{4,7},{5,6},{6,5},{7,4},{8,11},{9,10},{10,... | collective-permute-start | bytes 396296 | tf_op jit(solution)/shard_map/ppermute | solution.py:35
  31.8 7.8 %collective-permute-start.9 = (bf16[4,16512]{1,0:T(4,128)(2,1)S(1)}, bf16[4,16512]{1,0:T(4,128)(2,1)S(1)}, u32[]{:S(2)}, u32[]{:S(2)}) collective-permute-start(bf16[4,16512]{1,0:T(4,128)(2,1)S(1)} %get-tuple-element.28), channel_id=1, source_target_pairs={{0,5},{1,4},{2,7},{3,6},{4,1},{5,0},{6,3},{7,2},{8,13},{9,12},{10,... | collective-permute-start | bytes 396296 | tf_op jit(solution)/shard_map/ppermute | solution.py:35
  39.9 5.3 %collective-permute-start.11 = (bf16[1,16512]{1,0:T(2,128)(2,1)S(1)}, bf16[1,16512]{1,0:T(2,128)(2,1)S(1)}, u32[]{:S(2)}, u32[]{:S(2)}) collective-permute-start(bf16[1,16512]{1,0:T(2,128)(2,1)S(1)} %get-tuple-element.31), channel_id=1, source_target_pairs={{0,9},{1,8},{2,11},{3,10},{4,13},{5,12},{6,15},{7,14},{8,1},{9,0},... | collective-permute-start | bytes 99080 | tf_op jit(solution)/shard_map/ppermute | solution.py:35
  40.0 5.2 %collective-permute-start.12 = (bf16[1,16512]{1,0:T(2,128)(2,1)S(1)}, bf16[1,16512]{1,0:T(2,128)(2,1)S(1)}, u32[]{:S(2)}, u32[]{:S(2)}) collective-permute-start(bf16[1,16512]{1,0:T(2,128)(2,1)S(1)} %get-tuple-element.32), channel_id=1, source_target_pairs={{0,17},{1,16},{2,19},{3,18},{4,21},{5,20},{6,23},{7,22},{8,25},{9,... | collective-permute-start | bytes 99080 | tf_op jit(solution)/shard_map/ppermute | solution.py:35
  40.4 7.0 %collective-permute-start.13 = (bf16[1,16512]{1,0:T(2,128)(2,1)S(1)}, bf16[1,16512]{1,0:T(2,128)(2,1)S(1)}, u32[]{:S(2)}, u32[]{:S(2)}) collective-permute-start(bf16[1,16512]{1,0:T(2,128)(2,1)S(1)} %get-tuple-element.33), channel_id=1, source_target_pairs={{0,25},{1,24},{2,27},{3,26},{4,29},{5,28},{6,31},{7,30},{8,17},{9,... | collective-permute-start | bytes 99080 | tf_op jit(solution)/shard_map/ppermute | solution.py:35
